TPU v7x, 256 devices: a 8x8x2 block of a 8x8x16 slice. The times are simulated.
256 devices in a mesh: groups: 2 (over z), cells: 128 (over y, x, core).
Axes of the slice: x: 8, y: 8, z: 2, core: 2. Of those that a mesh axis runs over, the one named last changes fastest.
The devices are a block of a 8x8x16 slice.
Arguments:
- pair_act: bfloat16 [768, 384, 128], P(('groups', 'cells')), parts along dimension 0, may hold values from -6 to 6
- pair_mask: int32 [768, 384], P(('groups', 'cells')), parts along dimension 0, may hold values from 0 to 1, as said below
- chain_ids: int32 [768], P('groups'), parts along dimension 0, may hold values from 0 to 3, never falling along the last dimension, each value on 1 to 192 neighbouring positions
- proj_weight: bfloat16 [128, 256], replicated, may hold values from -0.5 to 0.5
- gate_weight: bfloat16 [128, 128], replicated, may hold values from -0.5 to 0.5
- chain_bias: float32 [2, 128], replicated, may hold values from -4 to 4
- out_weight: bfloat16 [64, 128], replicated, may hold values from -0.75 to 0.75
- out_grad: bfloat16 [768, 384, 128], P(('groups', 'cells')), parts along dimension 0, may hold values from -6 to 6
Outputs:
- pair_grad: bfloat16 [768, 384, 128], P(('groups', 'cells')), parts along dimension 0
- proj_weight_grad: float32 [256, 256], P('groups'), parts along dimension 0
- gate_weight_grad: float32 [256, 128], P('groups'), parts along dimension 0
- out_weight_grad: float32 [128, 128], P('groups'), parts along dimension 0
There are 2 independent parts, one for each index of `groups`. A program takes and returns all parts, laid end to end along the dimension named above; an argument that names none is the same for every part. Nothing has to cross between parts.
Inputs may be any that keep to these rules, and one draw needn't show every extreme that they name: pair_mask[i, j] = valid[i] * valid[j] for a 0 or 1 validity of each residue.
All inputs are finite; a program needn't handle non-finite values.
Results may differ from a plain program's by a relative error of at most 0.012.
Values may be sent and summed in bfloat16 or wider, within the bound.
A program may use at most 64 MiB of HBM per device.

v0:
```python
import jax
import jax.numpy as jnp
from jax import lax
from jax.sharding import PartitionSpec as P

EPS = 1e-05


def in_one(arrays, axis):
    ends = [0]
    for a in arrays:
        ends.append(ends[-1] + a.size)
    subtotal = lax.psum(jnp.concatenate([a.ravel() for a in arrays]), axis)
    return tuple((subtotal[b:e].reshape(a.shape) for a, b, e in zip(arrays, ends, ends[1:])))


def normalize_axis(values, axis):
    center = values - jnp.mean(values, axis=axis, keepdims=True)
    scale = lax.rsqrt(jnp.mean(center * center, axis=axis, keepdims=True) + EPS)
    return (center * scale, scale)


def norm_backward(grad, normed, scale, axis):
    first = jnp.mean(grad, axis=axis, keepdims=True)
    second = jnp.mean(grad * normed, axis=axis, keepdims=True)
    return scale * (grad - first - normed * second)


def local(
    pair_act, pair_mask, chain_ids, proj_weight, gate_weight, chain_bias, out_weight, out_grad
):
    devices = lax.axis_size("cells")
    rows_here = pair_act.shape[0]
    length = pair_act.shape[1]
    width = pair_act.shape[2]
    hidden = out_weight.shape[0]
    halfway = length // 2
    channel_pairs = devices // 2
    per_device = 2 * hidden // devices
    count = rows_here * length
    zfull = pair_act.astype(jnp.float32).reshape(count, width)
    zhat, zscale = normalize_axis(zfull, 1)
    normed = zhat.astype(jnp.bfloat16)
    projected = jnp.einsum("xc,cf->fx", normed, proj_weight, preferred_element_type=jnp.float32)
    keeper = pair_mask.astype(jnp.float32).reshape(1, count)
    values = projected[: 2 * hidden]
    sigma = jax.nn.sigmoid(projected[2 * hidden :])
    factors = (keeper * sigma * values).astype(jnp.bfloat16)
    outgoing = factors.reshape(2, channel_pairs, per_device, rows_here, 2, halfway)
    outgoing = jnp.transpose(outgoing, (1, 4, 0, 2, 3, 5)).reshape(
        devices, 2, per_device, rows_here, halfway
    )
    arrived = lax.all_to_all(outgoing, "cells", split_axis=0, concat_axis=3, tiled=True)
    left_half = arrived[0, 0]
    right_half = arrived[0, 1]
    partial_value = jnp.einsum(
        "cik,cjk->cij", left_half, right_half, preferred_element_type=jnp.float32
    )
    landed = lax.all_to_all(
        partial_value.reshape(per_device, devices, rows_here, length).astype(jnp.bfloat16),
        "cells",
        split_axis=1,
        concat_axis=0,
        tiled=True,
    ).astype(jnp.float32)
    landed = landed.reshape(channel_pairs, 2, per_device, rows_here, length)
    triangle = jnp.sum(landed, axis=1).reshape(hidden, count)
    tri_hat, tri_scale = normalize_axis(triangle, 0)
    tri_low = tri_hat.astype(jnp.bfloat16)
    outputs = jnp.einsum("hx,hc->xc", tri_low, out_weight, preferred_element_type=jnp.float32)
    start = lax.axis_index("cells") * rows_here
    own_chain = lax.dynamic_slice_in_dim(chain_ids, start, rows_here, 0)
    same_chain = (own_chain[:, None] == chain_ids[None, :]).reshape(count, 1)
    logits = jnp.dot(normed, gate_weight, preferred_element_type=jnp.float32)
    logits = logits + jnp.where(same_chain, chain_bias[0][None, :], chain_bias[1][None, :])
    gating = jax.nn.sigmoid(logits)
    upstream = out_grad.reshape(count, width).astype(jnp.float32)
    d_outputs = (upstream * gating).astype(jnp.bfloat16)
    d_logits = (upstream * outputs * gating * (1.0 - gating)).astype(jnp.bfloat16)
    out_term = jnp.einsum("hx,xc->hc", tri_low, d_outputs, preferred_element_type=jnp.float32)
    gate_term = jnp.einsum("xc,xd->cd", normed, d_logits, preferred_element_type=jnp.float32)
    d_hat = jnp.einsum("xc,hc->hx", d_outputs, out_weight, preferred_element_type=jnp.float32)
    d_tri = norm_backward(d_hat, tri_hat, tri_scale, 0).astype(jnp.bfloat16)
    doubled = jnp.broadcast_to(
        d_tri.reshape(channel_pairs, 1, per_device, rows_here, length),
        (channel_pairs, 2, per_device, rows_here, length),
    )
    whole = lax.all_to_all(
        doubled.reshape(devices, per_device, rows_here, length),
        "cells",
        split_axis=0,
        concat_axis=2,
        tiled=True,
    )[0]
    d_left = jnp.einsum("cij,cjk->cik", whole, right_half, preferred_element_type=jnp.float32)
    d_right = jnp.einsum("cij,cik->cjk", whole, left_half, preferred_element_type=jnp.float32)
    d_pair = jnp.stack([d_left, d_right]).astype(jnp.bfloat16)
    returned = lax.all_to_all(
        d_pair.reshape(2, per_device, devices, rows_here, halfway),
        "cells",
        split_axis=2,
        concat_axis=2,
        tiled=True,
    )
    returned = returned.reshape(2, per_device, channel_pairs, 2, rows_here, halfway)
    d_factors = (
        jnp.transpose(returned, (0, 2, 1, 4, 3, 5)).reshape(2 * hidden, count).astype(jnp.float32)
    )
    d_values = d_factors * keeper * sigma
    d_gates = d_factors * keeper * values * sigma * (1.0 - sigma)
    d_proj = jnp.concatenate([d_values, d_gates], axis=0).astype(jnp.bfloat16)
    proj_term = jnp.einsum("xc,fx->cf", normed, d_proj, preferred_element_type=jnp.float32)
    d_normed = jnp.einsum("fx,cf->xc", d_proj, proj_weight, preferred_element_type=jnp.float32)
    d_normed = d_normed + jnp.einsum(
        "xd,cd->xc", d_logits, gate_weight, preferred_element_type=jnp.float32
    )
    pair_grad = (
        norm_backward(d_normed, zhat, zscale, 1)
        .astype(jnp.bfloat16)
        .reshape(rows_here, length, width)
    )
    proj_sum, gate_sum, out_sum = in_one((proj_term, gate_term, out_term), "cells")
    factor = 1.0 / length
    return (pair_grad, proj_sum * factor, gate_sum * factor, out_sum * factor)


def solution(mesh):
    placed = (
        P(("groups", "cells"), None, None),
        P(("groups", "cells"), None),
        P("groups"),
        P(),
        P(),
        P(),
        P(),
        P(("groups", "cells"), None, None),
    )
    return jax.shard_map(
        local,
        mesh=mesh,
        in_specs=placed,
        out_specs=(
            P(("groups", "cells"), None, None),
            P("groups", None),
            P("groups", None),
            P("groups", None),
        ),
        check_vma=False,
    )
```

profile of v0, /device:TPU:513, one launch (start us, length us, event | category | flops | bytes accessed | tf_op | source)
XLA Modules:
  0.0 339.7 jit_solution(11828793296574214934)
XLA Ops:
  7.2 1.2 convert_reduce_fusion
  8.4 1.4 multiply_reduce_fusion.1
  10.5 1.3 fusion.15
  12.7 1.1 copy.41
  13.8 27.4 %all-to-all-start = ((bf16[128,2,1,3,192]{4,1,3,2,0:T(2,128)(2,1)}), bf16[128,2,1,3,192]{4,1,3,2,0:T(2,128)(2,1)S(1)}, u32[]{:S(2)}, u32[]{:S(2)}) async-start(bf16[128,2,1,3,192]{4,1,3,2,0:T(2,128)(2,1)} %bitcast.4), calls=%async_computation | async-start | bytes 786432 | tf_op jit(solution)/shard_map/all_to_all | solution.py:53
  41.3 17.2 %all-to-all-done = bf16[128,2,1,3,192]{4,1,3,2,0:T(2,128)(2,1)S(1)} async-done(((bf16[128,2,1,3,192]{4,1,3,2,0:T(2,128)(2,1)}), bf16[128,2,1,3,192]{4,1,3,2,0:T(2,128)(2,1)S(1)}, u32[]{:S(2)}, u32[]{:S(2)}) %all-to-all-start) | async-done | bytes 294944 | tf_op jit(solution)/shard_map/all_to_all | solution.py:53
  58.5 1.5 fusion.38
  61.2 1.0 copy.47
  62.2 7.6 %all-to-all-start.1 = ((bf16[1,128,3,384]{3,2,0,1:T(4,128)(2,1)}), bf16[1,128,3,384]{3,2,0,1:T(4,128)(2,1)S(1)}, u32[]{:S(2)}, u32[]{:S(2)}) async-start(bf16[1,128,3,384]{3,2,0,1:T(4,128)(2,1)} %copy.47), calls=%async_computation.1 | async-start | bytes 786432 | tf_op jit(solution)/shard_map/all_to_all | solution.py:59
  69.9 1.2 fusion.10
  71.1 15.6 %all-to-all-done.1 = bf16[1,128,3,384]{3,2,0,1:T(4,128)(2,1)S(1)} async-done(((bf16[1,128,3,384]{3,2,0,1:T(4,128)(2,1)}), bf16[1,128,3,384]{3,2,0,1:T(4,128)(2,1)S(1)}, u32[]{:S(2)}, u32[]{:S(2)}) %all-to-all-start.1) | async-done | bytes 294944 | tf_op jit(solution)/shard_map/all_to_all | solution.py:59
  87.8 0.9 broadcast_in_dim.53
  88.6 7.4 %all-to-all-start.2 = ((bf16[128,1,3,384]{3,2,1,0:T(4,128)(2,1)}), bf16[128,1,3,384]{3,2,1,0:T(4,128)(2,1)S(1)}, u32[]{:S(2)}, u32[]{:S(2)}) async-start(bf16[128,1,3,384]{3,2,1,0:T(4,128)(2,1)} %bitcast.18), calls=%async_computation.2 | async-start | bytes 786432 | tf_op jit(solution)/shard_map/all_to_all | solution.py:88
  96.8 16.4 %all-to-all-done.2 = bf16[128,1,3,384]{3,2,1,0:T(4,128)(2,1)S(1)} async-done(((bf16[128,1,3,384]{3,2,1,0:T(4,128)(2,1)}), bf16[128,1,3,384]{3,2,1,0:T(4,128)(2,1)S(1)}, u32[]{:S(2)}, u32[]{:S(2)}) %all-to-all-start.2) | async-done | bytes 294944 | tf_op jit(solution)/shard_map/all_to_all | solution.py:88
  114.4 1.2 copy.53
  115.6 7.4 %all-to-all-start.3 = ((bf16[2,1,128,3,192]{4,0,3,1,2:T(2,128)(2,1)}), bf16[2,1,128,3,192]{4,0,3,1,2:T(2,128)(2,1)S(1)}, u32[]{:S(2)}, u32[]{:S(2)}) async-start(bf16[2,1,128,3,192]{4,0,3,1,2:T(2,128)(2,1)} %copy.53), calls=%async_computation.3 | async-start | bytes 786432 | tf_op jit(solution)/shard_map/all_to_all | solution.py:98
  123.5 1.4 fusion.6
  125.2 14.9 %all-to-all-done.3 = bf16[2,1,128,3,192]{4,0,3,1,2:T(2,128)(2,1)S(1)} async-done(((bf16[2,1,128,3,192]{4,0,3,1,2:T(2,128)(2,1)}), bf16[2,1,128,3,192]{4,0,3,1,2:T(2,128)(2,1)S(1)}, u32[]{:S(2)}, u32[]{:S(2)}) %all-to-all-start.3) | async-done | bytes 294944 | tf_op jit(solution)/shard_map/all_to_all | solution.py:98
  142.6 0.7 fusion.37
  144.2 1.4 multiply_convert_fusion
  145.6 182.7 %all-reduce.2.cloned.1.call-done = f32[57344]{0:T(1024)} async-done(((f32[57344]{0:T(1024)}), f32[57344]{0:T(1024)}) %all-reduce.2.cloned.1.call-update) | async-done | bytes 229392 | tf_op jit(solution)/shard_map/psum | solution.py:13
  328.3 0.9 slice_multiply_fusion
  329.9 1.4 fusion.32
  331.3 1.5 fusion.31
  (71 shorter events, 10.5 us)
Async XLA Ops:
  7.2 4.6 %copy-start = (bf16[128,256]{1,0:T(8,128)(2,1)S(1)}, bf16[128,256]{1,0:T(8,128)(2,1)}, u32[]{:S(2)}) copy-start(bf16[128,256]{1,0:T(8,128)(2,1)} %param.11) | copy-start | bytes 196612
  12.4 28.9 %copy-start.8 = (s32[384]{0:T(512)S(1)}, s32[384]{0:T(512)}, u32[]{:S(2)}) copy-start(s32[384]{0:T(512)} %param.10) | copy-start | bytes 4612
  13.8 44.7 %all-to-all-start = ((bf16[128,2,1,3,192]{4,1,3,2,0:T(2,128)(2,1)}), bf16[128,2,1,3,192]{4,1,3,2,0:T(2,128)(2,1)S(1)}, u32[]{:S(2)}, u32[]{:S(2)}) async-start(bf16[128,2,1,3,192]{4,1,3,2,0:T(2,128)(2,1)} %bitcast.4), calls=%async_computation | async-start | bytes 786432 | tf_op jit(solution)/shard_map/all_to_all | solution.py:53
  60.8 9.1 %copy-start.9 = (f32[2,128]{1,0:T(2,128)S(1)}, f32[2,128]{1,0:T(2,128)}, u32[]{:S(2)}) copy-start(f32[2,128]{1,0:T(2,128)} %param.13) | copy-start | bytes 3076
  60.8 9.1 %copy-start.2 = (bf16[3,384,128]{2,1,0:T(8,128)(2,1)S(1)}, bf16[3,384,128]{2,1,0:T(8,128)(2,1)}, u32[]{:S(2)}) copy-start(bf16[3,384,128]{2,1,0:T(8,128)(2,1)} %param.15) | copy-start | bytes 884740
  60.8 9.1 %copy-start.6 = (bf16[128,128]{1,0:T(8,128)(2,1)S(1)}, bf16[128,128]{1,0:T(8,128)(2,1)}, u32[]{:S(2)}) copy-start(bf16[128,128]{1,0:T(8,128)(2,1)} %param.12) | copy-start | bytes 98308
  62.2 24.5 %all-to-all-start.1 = ((bf16[1,128,3,384]{3,2,0,1:T(4,128)(2,1)}), bf16[1,128,3,384]{3,2,0,1:T(4,128)(2,1)S(1)}, u32[]{:S(2)}, u32[]{:S(2)}) async-start(bf16[1,128,3,384]{3,2,0,1:T(4,128)(2,1)} %copy.47), calls=%async_computation.1 | async-start | bytes 786432 | tf_op jit(solution)/shard_map/all_to_all | solution.py:59
  71.1 16.3 %copy-start.4 = (bf16[64,128]{1,0:T(8,128)(2,1)S(1)}, bf16[64,128]{1,0:T(8,128)(2,1)}, u32[]{:S(2)}) copy-start(bf16[64,128]{1,0:T(8,128)(2,1)} %param.14) | copy-start | bytes 49156
  88.6 24.5 %all-to-all-start.2 = ((bf16[128,1,3,384]{3,2,1,0:T(4,128)(2,1)}), bf16[128,1,3,384]{3,2,1,0:T(4,128)(2,1)S(1)}, u32[]{:S(2)}, u32[]{:S(2)}) async-start(bf16[128,1,3,384]{3,2,1,0:T(4,128)(2,1)} %bitcast.18), calls=%async_computation.2 | async-start | bytes 786432 | tf_op jit(solution)/shard_map/all_to_all | solution.py:88
  114.4 9.1 %copy-start.3 = (bf16[3,384,128]{2,1,0:T(8,128)(2,1)S(1)}, bf16[3,384,128]{2,1,0:T(8,128)(2,1)}, u32[]{:S(2)}) copy-start(bf16[3,384,128]{2,1,0:T(8,128)(2,1)} %param.15) | copy-start | bytes 884740
  114.4 9.1 %copy-start.5 = (bf16[64,128]{1,0:T(8,128)(2,1)S(1)}, bf16[64,128]{1,0:T(8,128)(2,1)}, u32[]{:S(2)}) copy-start(bf16[64,128]{1,0:T(8,128)(2,1)} %param.14) | copy-start | bytes 49156
  115.6 24.5 %all-to-all-start.3 = ((bf16[2,1,128,3,192]{4,0,3,1,2:T(2,128)(2,1)}), bf16[2,1,128,3,192]{4,0,3,1,2:T(2,128)(2,1)S(1)}, u32[]{:S(2)}, u32[]{:S(2)}) async-start(bf16[2,1,128,3,192]{4,0,3,1,2:T(2,128)(2,1)} %copy.53), calls=%async_computation.3 | async-start | bytes 786432 | tf_op jit(solution)/shard_map/all_to_all | solution.py:98
  123.0 205.3 %all-reduce.2.cloned.1.call-start = ((), (), s32[]{:S(2)}) async-start(), calls=%async_computation.4 | async-start | bytes 458752 | tf_op jit(solution)/shard_map/psum | solution.py:13
  141.7 1.0 copy-start.1
  141.7 1.0 copy-start.7
Sparse Core Ops, SparseCore 0:
  144.3 183.9 all-reduce.1
where the time goes:
time: 340 us
  waiting for transfers between devices  247 us (73%)
  starting transfers between devices  50.2 us (15%)
  between operations  14.5 us (4%)
  other arithmetic  12 us (4%)
  local copies, waits for them, and re-layouts  10.4 us (3%)
  matrix products  5.81 us (2%)
    psum x1, waiting for transfers between devices, in_one(): subtotal = lax.psum(jnp.concatenate([a.ravel() for a in arrays]), axis)  183 us
    all_to_all x1, starting transfers between devices, local(): lax.all_to_all(outgoing, 'cells', split_axis=0, concat_axis=3, tiled=True)  27.4 us
    all_to_all x1, waiting for transfers between devices, local(): lax.all_to_all(outgoing, 'cells', split_axis=0, concat_axis=3, tiled=True)  17.2 us
    all_to_all x1, waiting for transfers between devices, local(): lax.all_to_all(doubled.reshape(devices, per_device, rows_here, length), '...  16.4 us
    all_to_all x1, waiting for transfers between devices, local(): lax.all_to_all(partial_value.reshape(per_device, devices, rows_here, leng...  15.6 us
    all_to_all x1, waiting for transfers between devices, local(): lax.all_to_all(d_pair.reshape(2, per_device, devices, rows_here, halfway)...  14.9 us
    all_to_all x1, starting transfers between devices, local(): lax.all_to_all(partial_value.reshape(per_device, devices, rows_here, leng...  7.62 us
    all_to_all x1, starting transfers between devices, local(): lax.all_to_all(d_pair.reshape(2, per_device, devices, rows_here, halfway)...  7.44 us
  transfers between devices with their start and end apart: 5, of which 5 were waited for; matrix products, arithmetic and copies ran while one was open for 2% of the time, Pallas kernels for 0%

commit v1 on v0

v1 whole, which is shorter than its diff:
```python
import jax
import jax.numpy as jnp
from jax import lax
from jax.experimental import pallas as pl
from jax.experimental.pallas import tpu as pltpu
from jax.sharding import PartitionSpec as P

EPS = 1e-05
MESH = pl.DeviceIdType.MESH
F32 = jnp.float32
BF16 = jnp.bfloat16
LANES = 128
NT = (((1,), (1,)), ((), ()))
TN = (((0,), (0,)), ((), ()))
NN = (((1,), (0,)), ((), ()))


def dot(a, b, dims):
    return lax.dot_general(a, b, dims, preferred_element_type=F32)


def loop(n, body, unroll=1):
    def step(i, carry):
        body(i)
        return carry

    lax.fori_loop(0, n, step, 0, unroll=unroll)


def kernel(
    act_ref,
    grad_ref,
    mask_ref,
    chain_ref,
    own_ref,
    proj_ref,
    gate_ref,
    bias_ref,
    outw_ref,
    pair_out,
    proj_out,
    gate_out,
    out_out,
    zhat_s,
    zscale_s,
    norm_s,
    p1_s,
    p2_s,
    do_s,
    e_s,
    dh_s,
    dl_s,
    dn_s,
    trilow_s,
    dproj_s,
    spread,
    wide,
    flat,
    a_s,
    b_s,
    dt_s,
    s1,
    r1,
    r1p,
    s2,
    r2,
    s3,
    r3,
    s4,
    r4,
    half_s,
    half_r,
    w_s,
    wp_r,
    ws,
    wr,
    gs,
    gr,
    wfin,
    wfin_r,
    send_sem,
    recv_sem,
    pair_send,
    pair_recv,
):
    me = lax.axis_index("cells")
    devices = lax.axis_size("cells")
    chips = devices // 2
    chip = me // 2
    core = lax.rem(me, 2)
    partner = me + 1 - 2 * core
    rows, length = mask_ref.shape[0], mask_ref.shape[2]
    width = act_ref.shape[1]
    hidden = outw_ref.shape[0]
    parts = length // LANES
    chunks = rows * parts
    tall = hidden // 8
    groups = chips // 8

    barrier = pltpu.get_barrier_semaphore()

    def greet(p):
        peer = lax.rem(chip + p + 1, chips) * 2 + core
        pl.semaphore_signal(barrier, inc=1, device_id={"cells": peer}, device_id_type=MESH)

    loop(chips - 1, greet)
    pl.semaphore_signal(barrier, inc=1, device_id={"cells": partner}, device_id_type=MESH)

    def exchange(src, dst, k):
        def one(p):
            t = lax.rem(chip + p + 1, chips)
            pltpu.make_async_remote_copy(
                src_ref=src.at[t],
                dst_ref=dst.at[chip],
                send_sem=send_sem.at[k],
                recv_sem=recv_sem.at[k],
                device_id={"cells": t * 2 + core},
                device_id_type=MESH,
            ).start()

        loop(chips - 1, one)
        pltpu.make_async_copy(src.at[chip], dst.at[chip], recv_sem.at[k]).start()

    def arrive(dst, k):
        pltpu.make_async_copy(dst, dst, recv_sem.at[k]).wait()

    def sent(src, k):
        view = src.at[pl.ds(0, chips - 1)]
        pltpu.make_async_copy(view, view, send_sem.at[k]).wait()

    def to_partner(src, dst, k):
        copy = pltpu.make_async_remote_copy(
            src_ref=src,
            dst_ref=dst,
            send_sem=pair_send.at[k],
            recv_sem=pair_recv.at[k],
            device_id={"cells": partner},
            device_id_type=MESH,
        )
        copy.start()
        return copy

    def cols(q):
        return pl.ds(pl.multiple_of(q * LANES, LANES), LANES)

    def unpack(src, dst):
        n = src.shape[1]

        def one(t):
            at = pl.ds(pl.multiple_of(t * 8, 8), n)
            for kq in range(parts):
                dst[kq, at, :] = src[t, :, kq * LANES : (kq + 1) * LANES].astype(F32)

        loop(chips, one, unroll=4)

    def pack(src, dst):
        n = dst.shape[1]

        def one(t):
            at = pl.ds(pl.multiple_of(t * 8, 8), n)
            for kq in range(parts):
                dst[t, :, kq * LANES : (kq + 1) * LANES] = src[kq, at, :].astype(BF16)

        loop(chips, one, unroll=4)

    def pack_rows(src, dst, at):
        def one(t):
            for kq in range(parts):
                dst[t, at : at + 4, kq * LANES : (kq + 1) * LANES] = src[
                    kq, pl.ds(t, 4, stride=chips), :
                ].astype(BF16)

        loop(chips, one, unroll=4)

    def gather_rows(src, offset, dst):
        for r in range(rows):
            for g in range(0, groups, 2):
                for kq in range(parts):
                    both = [
                        src[kq, pl.ds((g + e) * 64 + offset + r, 8, stride=8), :] for e in range(2)
                    ]
                    dst[
                        r * chips + g * 8 : r * chips + g * 8 + 16, kq * LANES : (kq + 1) * LANES
                    ] = jnp.concatenate(both, axis=0).astype(BF16)

    eye = (
        lax.broadcasted_iota(jnp.int32, (width, width), 0)
        == lax.broadcasted_iota(jnp.int32, (width, width), 1)
    ).astype(BF16)

    def front(q):
        r = q // parts
        kq = lax.rem(q, parts)
        z = dot(eye, act_ref[cols(q), :], NT)
        center = z - jnp.mean(z, axis=0, keepdims=True)
        scale = lax.rsqrt(jnp.mean(center * center, axis=0, keepdims=True) + EPS)
        zhat = center * scale
        low = zhat.astype(BF16)
        zhat_s[:, cols(q)] = zhat
        zscale_s[:, cols(q)] = scale
        norm_s[:, cols(q)] = low
        projected = dot(proj_ref[...], low, TN)
        keeper = mask_ref[r, :, cols(kq)].astype(F32)
        values = projected[: 2 * hidden]
        sigma = jax.nn.sigmoid(projected[2 * hidden :])
        p1 = keeper * sigma
        factors = p1 * values
        p1_s[:, cols(q)] = p1
        p2_s[:, cols(q)] = factors * (1.0 - sigma)
        for ab in range(2):
            for g in range(tall):
                at = ab * hidden + g * 8
                spread[kq, pl.ds(g * 64 + ab * 4 + r, 8, stride=8), :] = factors[at : at + 8]

    loop(chunks, front)
    pack(spread, s1)
    pl.semaphore_wait(barrier, chips)
    exchange(s1, r1, 0)

    def gating(q):
        r = q // parts
        kq = lax.rem(q, parts)
        same = chain_ref[:, cols(kq)] == own_ref[me * rows + r]
        logits = dot(gate_ref[...], norm_s[:, cols(q)], TN)
        logits = logits + jnp.where(same, bias_ref[:, 0:1], bias_ref[:, 1:2])
        gate = jax.nn.sigmoid(logits)
        up = dot(eye, grad_ref[cols(q), :], NT) * gate
        low = up.astype(BF16)
        do_s[:, cols(q)] = low
        e_s[:, cols(q)] = up * (1.0 - gate)
        dh_s[:, cols(q)] = dot(outw_ref[...], low, NN)

    loop(chunks, gating)

    arrive(r1, 0)
    first = to_partner(r1, r1p, 0)
    unpack(r1, spread)
    gather_rows(spread, 0, a_s)

    def place_right(src, which):
        for r in range(rows):
            for g in range(groups):
                for kq in range(parts):
                    wide[kq, pl.ds(g * 48 + 3 * which + r, 8, stride=6), :] = src[
                        kq, pl.ds(g * 64 + 4 + r, 8, stride=8), :
                    ]

    place_right(spread, core)
    first.wait()
    unpack(r1p, spread)
    place_right(spread, 1 - core)
    for kq in range(parts):
        b_s[:, kq * LANES : (kq + 1) * LANES] = wide[kq].astype(BF16)
    for kq in range(parts):
        flat[kq, : rows * chips, :] = dot(
            a_s[...], b_s[kq * LANES : (kq + 1) * LANES, :], NT
        )
    pack_rows(flat, s2, 0)
    exchange(s2, r2, 1)

    arrive(r2, 1)
    unpack(r2, spread)

    def middle(q):
        r = q // parts
        kq = lax.rem(q, parts)
        tri = jnp.concatenate(
            [spread[kq, pl.ds(g * 64 + r, 8, stride=8), :] for g in range(tall)], axis=0
        )
        center = tri - jnp.mean(tri, axis=0, keepdims=True)
        scale = lax.rsqrt(jnp.mean(center * center, axis=0, keepdims=True) + EPS)
        hat = center * scale
        low = hat.astype(BF16)
        trilow_s[:, cols(q)] = low
        outputs = dot(outw_ref[...], low, TN)
        dl_s[:, cols(q)] = (outputs * e_s[:, cols(q)]).astype(BF16)
        d_hat = dh_s[:, cols(q)]
        m1 = jnp.mean(d_hat, axis=0, keepdims=True)
        m2 = jnp.mean(d_hat * hat, axis=0, keepdims=True)
        d_tri = scale * (d_hat - m1 - hat * m2)
        for g in range(tall):
            spread[kq, pl.ds(g * 64 + 4 + r, 8, stride=8), :] = d_tri[g * 8 : g * 8 + 8]

    loop(chunks, middle)

    def pack_upper(t):
        at = pl.ds(pl.multiple_of(t * 8, 8), 8)
        for kq in range(parts):
            s3[t, :, kq * LANES : (kq + 1) * LANES] = spread[kq, at, :][4:8].astype(BF16)

    loop(chips, pack_upper, unroll=4)
    exchange(s3, r3, 2)

    w_s[0:width, :] = dot(norm_s[...], dl_s[...], NT)
    w_s[width : width + hidden, :] = dot(trilow_s[...], do_s[...], NT)
    w_s[width + hidden : 2 * width, :] = jnp.zeros((width - hidden, width), F32)

    def gate_part(q):
        dn_s[:, cols(q)] = dot(gate_ref[...], dl_s[:, cols(q)], NN)

    loop(chunks, gate_part)

    arrive(r3, 2)
    unpack(r3, spread)
    gather_rows(spread, 0, dt_s)
    for kq in range(parts):
        wide[kq] = dot(dt_s[...], a_s[:, kq * LANES : (kq + 1) * LANES], TN)
    for r in range(rows):
        for g in range(groups):
            for kq in range(parts):
                half_s[kq, r * chips + g * 8 : r * chips + g * 8 + 8, :] = wide[
                    kq, pl.ds(g * 48 + 3 * (1 - core) + r, 8, stride=6), :
                ]
    second = to_partner(half_s, half_r, 1)
    for kq in range(parts):
        flat[kq, : rows * chips, :] = dot(
            dt_s[...], b_s[:, kq * LANES : (kq + 1) * LANES], NN
        )
    pack_rows(flat, s4, 0)
    second.wait()
    for r in range(rows):
        for g in range(groups):
            for kq in range(parts):
                at = slice(r * chips + g * 8, r * chips + g * 8 + 8)
                flat[kq, at, :] = (
                    wide[kq, pl.ds(g * 48 + 3 * core + r, 8, stride=6), :] + half_r[kq, at, :]
                )
    pack_rows(flat, s4, 4)
    exchange(s4, r4, 3)

    arrive(r4, 3)
    unpack(r4, spread)

    def factor_back(q):
        r = q // parts
        kq = lax.rem(q, parts)
        d_factors = jnp.concatenate(
            [
                spread[kq, pl.ds(g * 64 + ab * 4 + r, 8, stride=8), :]
                for ab in range(2)
                for g in range(tall)
            ],
            axis=0,
        )
        dproj_s[: 2 * hidden, cols(q)] = (d_factors * p1_s[:, cols(q)]).astype(BF16)
        dproj_s[2 * hidden :, cols(q)] = (d_factors * p2_s[:, cols(q)]).astype(BF16)

    loop(chunks, factor_back)
    for e in range(2):
        w_s[2 * width + e * width : 3 * width + e * width, :] = dot(
            norm_s[...], dproj_s[e * width : (e + 1) * width, :], NT
        )

    quarter = 4 * chips
    here = pl.ds(pl.multiple_of(core * quarter, 8), quarter)
    there = pl.ds(pl.multiple_of((1 - core) * quarter, 8), quarter)
    third = to_partner(w_s.at[there], wp_r, 2)

    def finish(q):
        d_norm = dot(proj_ref[...], dproj_s[:, cols(q)], NN) + dn_s[:, cols(q)]
        zhat = zhat_s[:, cols(q)]
        m1 = jnp.mean(d_norm, axis=0, keepdims=True)
        m2 = jnp.mean(d_norm * zhat, axis=0, keepdims=True)
        grad = zscale_s[:, cols(q)] * (d_norm - m1 - zhat * m2)
        pair_out[cols(q), :] = grad.T.astype(BF16)

    third.wait()
    wp_r[...] = w_s[here, :] + wp_r[...]

    def split(t):
        ws[t] = wp_r[pl.ds(t, 4, stride=chips), :]

    loop(chips, split, unroll=4)
    exchange(ws, wr, 4)
    loop(chunks, finish)
    arrive(wr, 4)
    total = jnp.sum(wr[...], axis=0) * (1.0 / length)
    gs[...] = total

    def spread_total(p):
        t = lax.rem(chip + p + 1, chips)
        pltpu.make_async_remote_copy(
            src_ref=gs,
            dst_ref=gr.at[chip],
            send_sem=send_sem.at[5],
            recv_sem=recv_sem.at[5],
            device_id={"cells": t * 2 + core},
            device_id_type=MESH,
        ).start()

    loop(chips - 1, spread_total)
    pltpu.make_async_copy(gs, gr.at[chip], recv_sem.at[5]).start()
    arrive(gr, 5)

    def join(t):
        wfin[pl.ds(t, 4, stride=chips), :] = gr[t]

    loop(chips, join, unroll=4)
    last = to_partner(wfin, wfin_r, 3)
    last.wait()

    def emit(low, high):
        gate_out[...] = low[0:width, :]
        out_out[...] = low[width : width + hidden, :]
        for e in range(2):
            proj_out[:, e * width : (e + 1) * width] = high[e * width : (e + 1) * width, :]

    low = jnp.where(core == 0, wfin[...], wfin_r[...])
    high = jnp.where(core == 0, wfin_r[...], wfin[...])
    emit(low, high)

    sent(s1, 0)
    sent(s2, 1)
    sent(s3, 2)
    sent(s4, 3)
    sent(ws, 4)
    view = gr.at[pl.ds(0, chips - 1)]
    pltpu.make_async_copy(view, view, send_sem.at[5]).wait()


def local(
    pair_act, pair_mask, chain_ids, proj_weight, gate_weight, chain_bias, out_weight, out_grad
):
    devices = lax.axis_size("cells")
    chips = devices // 2
    rows, length, width = pair_act.shape
    hidden = out_weight.shape[0]
    count = rows * length
    parts = length // LANES
    vm = pl.BlockSpec(memory_space=pltpu.VMEM)
    sm = pl.BlockSpec(memory_space=pltpu.SMEM)
    V = pltpu.VMEM
    eight, four = (chips, 8, length), (chips, 4, length)
    out = pl.pallas_call(
        kernel,
        out_shape=(
            jax.ShapeDtypeStruct((count, width), BF16),
            jax.ShapeDtypeStruct((width, 4 * hidden), F32),
            jax.ShapeDtypeStruct((width, width), F32),
            jax.ShapeDtypeStruct((hidden, width), F32),
        ),
        in_specs=[vm, vm, vm, vm, sm, vm, vm, vm, vm],
        out_specs=(vm, vm, vm, vm),
        scratch_shapes=[
            V((width, count), F32),
            V((1, count), F32),
            V((width, count), BF16),
            V((2 * hidden, count), F32),
            V((2 * hidden, count), F32),
            V((width, count), BF16),
            V((width, count), F32),
            V((hidden, count), F32),
            V((width, count), BF16),
            V((width, count), F32),
            V((hidden, count), BF16),
            V((4 * hidden, count), BF16),
            V((parts, 8 * chips, LANES), F32),
            V((parts, length, LANES), F32),
            V((parts, 4 * chips, LANES), F32),
            V((rows * chips, length), BF16),
            V((length, length), BF16),
            V((rows * chips, length), BF16),
            V(eight, BF16),
            V(eight, BF16),
            V(eight, BF16),
            V(four, BF16),
            V(four, BF16),
            V(four, BF16),
            V(four, BF16),
            V(eight, BF16),
            V(eight, BF16),
            V((parts, rows * chips, LANES), F32),
            V((parts, rows * chips, LANES), F32),
            V((4 * width, width), F32),
            V((4 * chips, width), F32),
            V((chips, 4, width), F32),
            V((chips, 4, width), F32),
            V((4, width), F32),
            V((chips, 4, width), F32),
            V((4 * chips, width), F32),
            V((4 * chips, width), F32),
            pltpu.SemaphoreType.DMA((6,)),
            pltpu.SemaphoreType.DMA((6,)),
            pltpu.SemaphoreType.DMA((4,)),
            pltpu.SemaphoreType.DMA((4,)),
        ],
        compiler_params=pltpu.CompilerParams(
            collective_id=0, has_side_effects=True, vmem_limit_bytes=60 * 1024 * 1024
        ),
    )(
        pair_act.reshape(count, width),
        out_grad.reshape(count, width),
        pair_mask.reshape(rows, 1, length),
        chain_ids.reshape(1, length),
        chain_ids,
        proj_weight,
        gate_weight,
        chain_bias.T,
        out_weight,
    )
    return (out[0].reshape(rows, length, width), out[1], out[2], out[3])


def solution(mesh):
    placed = (
        P(("groups", "cells"), None, None),
        P(("groups", "cells"), None),
        P("groups"),
        P(),
        P(),
        P(),
        P(),
        P(("groups", "cells"), None, None),
    )
    return jax.shard_map(
        local,
        mesh=mesh,
        in_specs=placed,
        out_specs=(
            P(("groups", "cells"), None, None),
            P("groups", None),
            P("groups", None),
            P("groups", None),
        ),
        check_vma=False,
    )
```

time: 340 us -> 104 us (0.31)
  waiting for transfers between devices: 247 us -> 0 us
  Pallas kernels: 0 us -> 95.7 us
  starting transfers between devices: 50.2 us -> 0 us
  between operations: 14.5 us -> 0.66 us
  other arithmetic: 12 us -> 0 us
  matrix products: 5.81 us -> 0 us
    psum x1 -> x0, waiting for transfers between devices: 183 us -> none  [in_one(): subtotal = lax.psum(jnp.concatenate([a.ravel() for a in arrays]), axis)]
    pallas_call x0 -> x1, Pallas kernels: none -> 95.7 us  [local(): pl.pallas_call(kernel, out_shape=(jax.ShapeDtypeStruct((count, width), BF...]
    all_to_all x4 -> x0, waiting for transfers between devices: 64.1 us -> none  [the longest x1 17.2 us: local(): lax.all_to_all(outgoing, 'cells', split_axis=0, concat_axis=3, tiled=True)]
    all_to_all x4 -> x0, starting transfers between devices: 49.9 us -> none  [the longest x1 27.4 us: local(): lax.all_to_all(outgoing, 'cells', split_axis=0, concat_axis=3, tiled=True)]
    dot_general x12 -> x0, matrix products: 5.81 us -> none  [the longest x1 1.37 us: local(): jnp.einsum('hx,hc->xc', tri_low, out_weight, preferred_element_type=jnp.f...]
    convert_element_type x6 -> x0, other arithmetic: 3.93 us -> none  [the longest x1 1.39 us: local(): pair_grad = norm_backward(d_normed, zhat, zscale, 1).astype(jnp.bfloat16)...]
    mul x3 -> x0, other arithmetic: 3.77 us -> none  [local(): return (pair_grad, proj_sum * factor, gate_sum * factor, out_sum * factor)]
    unnamed x24 -> x15, local copies, waits for them, and re-layouts: 1.74 us -> 5.39 us
  transfers between devices with their start and end apart: 5 -> 0, of which waited for: 5 -> 0; matrix products, arithmetic and copies ran while one was open for 2% -> 0% of each run, Pallas kernels for 0% -> 0%
where the time goes in v1:
time: 104 us
  Pallas kernels  95.7 us (92%)
  local copies, waits for them, and re-layouts  7.25 us (7%)
    pallas_call x1, Pallas kernels, local(): pl.pallas_call(kernel, out_shape=(jax.ShapeDtypeStruct((count, width), BF...  95.7 us
    unnamed x15, local copies, waits for them, and re-layouts  5.39 us

profile of v1, /device:TPU:513, one launch (start us, length us, event | category | flops | bytes accessed | tf_op | source)
XLA Modules:
  0.0 103.6 jit_solution(13191157773054241994)
XLA Ops:
  0.6 0.0 copy-start.3
  0.6 0.7 copy-done.3
  1.3 0.6 reshape.26.chain_ref
  1.9 0.0 copy-start.4
  1.9 1.3 %reshape.25.mask_ref = s32[3,1,384]{2,1,0:T(1,128)} reshape(s32[3,384]{1,0:T(4,128)} %param.9) | data formatting | bytes 9216 | tf_op jit(solution)/shard_map/reshape | solution.py:493
  3.2 0.0 copy-done.4
  3.2 0.7 copy.12
  3.9 95.7 %shard_map.111 = (bf16[1152,128]{1,0:T(8,128)(2,1)}, f32[128,256]{1,0:T(8,128)}, f32[128,128]{1,0:T(8,128)}, f32[64,128]{1,0:T(8,128)}) custom-call(bf16[1152,128]{1,0:T(8,128)(2,1)} %bitcast.4, bf16[1152,128]{1,0:T(8,128)(2,1)} %bitcast.5, s32[3,1,384]{2,1,0:T(1,128)} %reshape.25.mask_ref, s32[1,384]{1,0:T(1,128)} %reshape.26.chain_ref, s32[384]{0:T(512)} %own_ref.1, ...), custom_call_target="tpu_custom_call" | custom-call | tf_op jit(solution)/shard_map/pallas_call | solution.py:434
  99.6 0.0 copy-start
  99.7 1.7 %copy.17 = bf16[3,384,128]{2,1,0:T(8,128)(2,1)} copy(bf16[3,384,128]{2,1,0:T(8,128)(2,1)} %bitcast.6) | data formatting | bytes 589824
  101.4 0.0 copy-done
  101.4 0.0 copy-start.1
  101.4 0.7 copy.18
  102.0 0.2 copy-done.1
  102.3 0.0 copy-start.2
  102.3 0.6 copy.19
  102.9 0.1 copy-done.2
  103.0 0.6 copy.20
Async XLA Ops:
  0.6 0.7 copy-start.3
  1.9 1.3 %copy-start.4 = (f32[2,128]{1,0:T(2,128)S(1)}, f32[2,128]{1,0:T(2,128)}, u32[]{:S(2)}) copy-start(f32[2,128]{1,0:T(2,128)} %param.13) | copy-start | bytes 3076
  99.6 1.7 %copy-start = (f32[128,256]{1,0:T(8,128)S(1)}, f32[128,256]{1,0:T(8,128)}, u32[]{:S(2)}) copy-start(f32[128,256]{1,0:T(8,128)} %get-tuple-element.17) | copy-start | bytes 393220
  101.4 0.9 copy-start.1
  102.3 0.8 copy-start.2

commit v2 on v1

--- a/solution.py
+++ b/solution.py
@@ -1,3 +1,5 @@
+import math
+
 import jax
 import jax.numpy as jnp
 from jax import lax
@@ -70,26 +72,35 @@
     r4,
     half_s,
     half_r,
-    w_s,
-    wp_r,
-    ws,
-    wr,
-    gs,
-    gr,
-    wfin,
-    wfin_r,
+    w1,
+    line1,
+    mid1a,
+    column1,
+    mid1b,
+    full1,
+    w2,
+    line2,
+    mid2a,
+    column2,
+    mid2b,
+    full2,
     send_sem,
     recv_sem,
     pair_send,
     pair_recv,
+    line_send,
+    line_recv,
 ):
     me = lax.axis_index("cells")
     devices = lax.axis_size("cells")
     chips = devices // 2
+    side = math.isqrt(chips)
     chip = me // 2
     core = lax.rem(me, 2)
+    row, col = chip // side, lax.rem(chip, side)
+    far = sorted(range(side), key=lambda d: -min(d, side - d))
     partner = me + 1 - 2 * core
-    rows, length = mask_ref.shape[0], mask_ref.shape[2]
+    rows, length = mask_ref.shape
     width = act_ref.shape[1]
     hidden = outw_ref.shape[0]
     parts = length // LANES
@@ -99,16 +110,27 @@
 
     barrier = pltpu.get_barrier_semaphore()
 
-    def greet(p):
-        peer = lax.rem(chip + p + 1, chips) * 2 + core
+    def each_chip(fn):
+        def line(i):
+            step = side // 2 + ((i + 1) // 2) * (1 - 2 * lax.rem(i, 2))
+            base = lax.rem(row + step, side) * side
+            for d in far:
+                fn(base + lax.rem(col + d, side))
+
+        loop(side - 1, line)
+        for d in far[:-1]:
+            fn(row * side + lax.rem(col + d, side))
+
+    def greet(peer):
         pl.semaphore_signal(barrier, inc=1, device_id={"cells": peer}, device_id_type=MESH)
 
-    loop(chips - 1, greet)
-    pl.semaphore_signal(barrier, inc=1, device_id={"cells": partner}, device_id_type=MESH)
+    each_chip(lambda t: greet(t * 2 + core))
+    for d in far[:-1]:
+        greet((row * side + lax.rem(col + d, side)) * 2 + 1 - core)
+    greet(partner)
 
     def exchange(src, dst, k):
-        def one(p):
-            t = lax.rem(chip + p + 1, chips)
+        def one(t):
             pltpu.make_async_remote_copy(
                 src_ref=src.at[t],
                 dst_ref=dst.at[chip],
@@ -118,7 +140,7 @@
                 device_id_type=MESH,
             ).start()
 
-        loop(chips - 1, one)
+        each_chip(one)
         pltpu.make_async_copy(src.at[chip], dst.at[chip], recv_sem.at[k]).start()
 
     def arrive(dst, k):
@@ -140,8 +162,12 @@
         copy.start()
         return copy
 
-    def cols(q):
-        return pl.ds(pl.multiple_of(q * LANES, LANES), LANES)
+    def cols(kq, r=0):
+        return pl.ds(pl.multiple_of((r * parts + kq) * LANES, LANES), LANES)
+
+    def cells(body, unroll=1):
+        for r in range(rows):
+            loop(parts, lambda kq, r=r: body(r, kq), unroll)
 
     def unpack(src, dst):
         n = src.shape[1]
@@ -188,49 +214,50 @@
         == lax.broadcasted_iota(jnp.int32, (width, width), 1)
     ).astype(BF16)
 
-    def front(q):
-        r = q // parts
-        kq = lax.rem(q, parts)
-        z = dot(eye, act_ref[cols(q), :], NT)
+    def front(r, kq):
+        q = cols(kq, r)
+        z = dot(eye, act_ref[q, :], NT)
         center = z - jnp.mean(z, axis=0, keepdims=True)
         scale = lax.rsqrt(jnp.mean(center * center, axis=0, keepdims=True) + EPS)
         zhat = center * scale
         low = zhat.astype(BF16)
-        zhat_s[:, cols(q)] = zhat
-        zscale_s[:, cols(q)] = scale
-        norm_s[:, cols(q)] = low
+        zhat_s[:, q] = zhat
+        zscale_s[:, q] = scale
+        norm_s[:, q] = low
         projected = dot(proj_ref[...], low, TN)
-        keeper = mask_ref[r, :, cols(kq)].astype(F32)
+        keeper = mask_ref[r : r + 1, cols(kq)].astype(F32)
         values = projected[: 2 * hidden]
         sigma = jax.nn.sigmoid(projected[2 * hidden :])
         p1 = keeper * sigma
         factors = p1 * values
-        p1_s[:, cols(q)] = p1
-        p2_s[:, cols(q)] = factors * (1.0 - sigma)
+        p1_s[:, q] = p1
+        p2_s[:, q] = factors * (1.0 - sigma)
         for ab in range(2):
             for g in range(tall):
                 at = ab * hidden + g * 8
                 spread[kq, pl.ds(g * 64 + ab * 4 + r, 8, stride=8), :] = factors[at : at + 8]
 
-    loop(chunks, front)
+    cells(front, unroll=3)
     pack(spread, s1)
-    pl.semaphore_wait(barrier, chips)
+    pl.semaphore_wait(barrier, chips + side - 1)
     exchange(s1, r1, 0)
 
-    def gating(q):
-        r = q // parts
-        kq = lax.rem(q, parts)
-        same = chain_ref[:, cols(kq)] == own_ref[me * rows + r]
-        logits = dot(gate_ref[...], norm_s[:, cols(q)], TN)
-        logits = logits + jnp.where(same, bias_ref[:, 0:1], bias_ref[:, 1:2])
+    within, across = (
+        jnp.sum(eye.astype(F32) * bias_ref[e : e + 1, :], axis=1, keepdims=True) for e in range(2)
+    )
+    def gating(r, kq):
+        q = cols(kq, r)
+        same = chain_ref[cols(kq)].reshape(1, LANES) == own_ref[me * rows + r]
+        logits = dot(gate_ref[...], norm_s[:, q], TN)
+        logits = logits + jnp.where(same, within, across)
         gate = jax.nn.sigmoid(logits)
-        up = dot(eye, grad_ref[cols(q), :], NT) * gate
+        up = dot(eye, grad_ref[q, :], NT) * gate
         low = up.astype(BF16)
-        do_s[:, cols(q)] = low
-        e_s[:, cols(q)] = up * (1.0 - gate)
-        dh_s[:, cols(q)] = dot(outw_ref[...], low, NN)
-
-    loop(chunks, gating)
+        do_s[:, q] = low
+        e_s[:, q] = up * (1.0 - gate)
+        dh_s[:, q] = dot(outw_ref[...], low, NN)
+
+    cells(gating, unroll=3)
 
     arrive(r1, 0)
     first = to_partner(r1, r1p, 0)
@@ -261,9 +288,8 @@
     arrive(r2, 1)
     unpack(r2, spread)
 
-    def middle(q):
-        r = q // parts
-        kq = lax.rem(q, parts)
+    def middle(r, kq):
+        q = cols(kq, r)
         tri = jnp.concatenate(
             [spread[kq, pl.ds(g * 64 + r, 8, stride=8), :] for g in range(tall)], axis=0
         )
@@ -271,17 +297,17 @@
         scale = lax.rsqrt(jnp.mean(center * center, axis=0, keepdims=True) + EPS)
         hat = center * scale
         low = hat.astype(BF16)
-        trilow_s[:, cols(q)] = low
+        trilow_s[:, q] = low
         outputs = dot(outw_ref[...], low, TN)
-        dl_s[:, cols(q)] = (outputs * e_s[:, cols(q)]).astype(BF16)
-        d_hat = dh_s[:, cols(q)]
+        dl_s[:, q] = (outputs * e_s[:, q]).astype(BF16)
+        d_hat = dh_s[:, q]
         m1 = jnp.mean(d_hat, axis=0, keepdims=True)
         m2 = jnp.mean(d_hat * hat, axis=0, keepdims=True)
         d_tri = scale * (d_hat - m1 - hat * m2)
         for g in range(tall):
             spread[kq, pl.ds(g * 64 + 4 + r, 8, stride=8), :] = d_tri[g * 8 : g * 8 + 8]
 
-    loop(chunks, middle)
+    cells(middle, unroll=3)
 
     def pack_upper(t):
         at = pl.ds(pl.multiple_of(t * 8, 8), 8)
@@ -291,14 +317,65 @@
     loop(chips, pack_upper, unroll=4)
     exchange(s3, r3, 2)
 
-    w_s[0:width, :] = dot(norm_s[...], dl_s[...], NT)
-    w_s[width : width + hidden, :] = dot(trilow_s[...], do_s[...], NT)
-    w_s[width + hidden : 2 * width, :] = jnp.zeros((width - hidden, width), F32)
-
-    def gate_part(q):
-        dn_s[:, cols(q)] = dot(gate_ref[...], dl_s[:, cols(q)], NN)
-
-    loop(chunks, gate_part)
+    share = 2 * side
+    spot = col * 2 + core
+    block = w1.shape[0] // share
+
+    def own(m):
+        return pl.ds(pl.multiple_of(m * block, block), block)
+
+    def line_peers(fn):
+        for d in far:
+            for e in range(2):
+                if d or e:
+                    fn((row * side + lax.rem(col + d, side)) * 2 + (1 - core if e else core))
+
+    def send(src, dst, k, device):
+        pltpu.make_async_remote_copy(
+            src_ref=src,
+            dst_ref=dst,
+            send_sem=line_send.at[k],
+            recv_sem=line_recv.at[k],
+            device_id={"cells": device},
+            device_id_type=MESH,
+        ).start()
+
+    def scatter_line(src, dst, k):
+        line_peers(lambda p: send(src.at[own(lax.rem(p, share))], dst.at[spot], k, p))
+        pltpu.make_async_copy(src.at[own(spot)], dst.at[spot], line_recv.at[k]).start()
+
+    def reduce_column(src, mid, dst, k):
+        pltpu.make_async_copy(src, src, line_recv.at[k - 1]).wait()
+        mid[...] = jnp.sum(src[...].astype(F32), axis=0)
+        for d in far[:-1]:
+            p = (lax.rem(row + d, side) * side + col) * 2 + core
+            send(mid, dst.at[row], k, p)
+        pltpu.make_async_copy(mid, dst.at[row], line_recv.at[k]).start()
+
+    def gather_line(src, mid, dst, k):
+        pltpu.make_async_copy(src, src, line_recv.at[k - 1]).wait()
+        mid[...] = jnp.sum(src[...], axis=0) * (1.0 / length)
+        line_peers(lambda p: send(mid, dst.at[own(spot)], k, p))
+        pltpu.make_async_copy(mid, dst.at[own(spot)], line_recv.at[k]).start()
+
+    def drain(w, mid, dst, k):
+        view = w.at[pl.ds(0, (share - 1) * block)]
+        pltpu.make_async_copy(view, view, line_send.at[k]).wait()
+        view = dst.at[pl.ds(0, (side - 1) * block)]
+        pltpu.make_async_copy(view, view, line_send.at[k + 1]).wait()
+        view = dst.at[pl.ds(0, (share - 1) * block)]
+        pltpu.make_async_copy(view, view, line_send.at[k + 2]).wait()
+
+    w1[0:width, :] = dot(norm_s[...], dl_s[...], NT).astype(BF16)
+    w1[width : width + hidden, :] = dot(trilow_s[...], do_s[...], NT).astype(BF16)
+    w1[width + hidden : 2 * width, :] = jnp.zeros((width - hidden, width), BF16)
+    scatter_line(w1, line1, 0)
+
+    def gate_part(r, kq):
+        q = cols(kq, r)
+        dn_s[:, q] = dot(gate_ref[...], dl_s[:, q], NN)
+
+    cells(gate_part, unroll=3)
 
     arrive(r3, 2)
     unpack(r3, spread)
@@ -327,13 +404,13 @@
                 )
     pack_rows(flat, s4, 4)
     exchange(s4, r4, 3)
+    reduce_column(line1, mid1a, column1, 1)
 
     arrive(r4, 3)
     unpack(r4, spread)
 
-    def factor_back(q):
-        r = q // parts
-        kq = lax.rem(q, parts)
+    def factor_back(r, kq):
+        q = cols(kq, r)
         d_factors = jnp.concatenate(
             [
                 spread[kq, pl.ds(g * 64 + ab * 4 + r, 8, stride=8), :]
@@ -342,80 +419,41 @@
             ],
             axis=0,
         )
-        dproj_s[: 2 * hidden, cols(q)] = (d_factors * p1_s[:, cols(q)]).astype(BF16)
-        dproj_s[2 * hidden :, cols(q)] = (d_factors * p2_s[:, cols(q)]).astype(BF16)
-
-    loop(chunks, factor_back)
+        dproj_s[: 2 * hidden, q] = (d_factors * p1_s[:, q]).astype(BF16)
+        dproj_s[2 * hidden :, q] = (d_factors * p2_s[:, q]).astype(BF16)
+
+    cells(factor_back, unroll=3)
     for e in range(2):
-        w_s[2 * width + e * width : 3 * width + e * width, :] = dot(
+        w2[e * width : (e + 1) * width, :] = dot(
             norm_s[...], dproj_s[e * width : (e + 1) * width, :], NT
-        )
-
-    quarter = 4 * chips
-    here = pl.ds(pl.multiple_of(core * quarter, 8), quarter)
-    there = pl.ds(pl.multiple_of((1 - core) * quarter, 8), quarter)
-    third = to_partner(w_s.at[there], wp_r, 2)
-
-    def finish(q):
-        d_norm = dot(proj_ref[...], dproj_s[:, cols(q)], NN) + dn_s[:, cols(q)]
-        zhat = zhat_s[:, cols(q)]
+        ).astype(BF16)
+    scatter_line(w2, line2, 3)
+    gather_line(column1, mid1b, full1, 2)
+
+    def finish(r, kq):
+        q = cols(kq, r)
+        d_norm = dot(proj_ref[...], dproj_s[:, q], NN) + dn_s[:, q]
+        zhat = zhat_s[:, q]
         m1 = jnp.mean(d_norm, axis=0, keepdims=True)
         m2 = jnp.mean(d_norm * zhat, axis=0, keepdims=True)
-        grad = zscale_s[:, cols(q)] * (d_norm - m1 - zhat * m2)
-        pair_out[cols(q), :] = grad.T.astype(BF16)
-
-    third.wait()
-    wp_r[...] = w_s[here, :] + wp_r[...]
-
-    def split(t):
-        ws[t] = wp_r[pl.ds(t, 4, stride=chips), :]
-
-    loop(chips, split, unroll=4)
-    exchange(ws, wr, 4)
-    loop(chunks, finish)
-    arrive(wr, 4)
-    total = jnp.sum(wr[...], axis=0) * (1.0 / length)
-    gs[...] = total
-
-    def spread_total(p):
-        t = lax.rem(chip + p + 1, chips)
-        pltpu.make_async_remote_copy(
-            src_ref=gs,
-            dst_ref=gr.at[chip],
-            send_sem=send_sem.at[5],
-            recv_sem=recv_sem.at[5],
-            device_id={"cells": t * 2 + core},
-            device_id_type=MESH,
-        ).start()
-
-    loop(chips - 1, spread_total)
-    pltpu.make_async_copy(gs, gr.at[chip], recv_sem.at[5]).start()
-    arrive(gr, 5)
-
-    def join(t):
-        wfin[pl.ds(t, 4, stride=chips), :] = gr[t]
-
-    loop(chips, join, unroll=4)
-    last = to_partner(wfin, wfin_r, 3)
-    last.wait()
-
-    def emit(low, high):
-        gate_out[...] = low[0:width, :]
-        out_out[...] = low[width : width + hidden, :]
-        for e in range(2):
-            proj_out[:, e * width : (e + 1) * width] = high[e * width : (e + 1) * width, :]
-
-    low = jnp.where(core == 0, wfin[...], wfin_r[...])
-    high = jnp.where(core == 0, wfin_r[...], wfin[...])
-    emit(low, high)
-
+        grad = zscale_s[:, q] * (d_norm - m1 - zhat * m2)
+        pair_out[q, :] = grad.T.astype(BF16)
+
+    cells(finish, unroll=3)
+    reduce_column(line2, mid2a, column2, 4)
+    gather_line(column2, mid2b, full2, 5)
+    pltpu.make_async_copy(full1, full1, line_recv.at[2]).wait()
+    gate_out[...] = full1[0:width, :]
+    out_out[...] = full1[width : width + hidden, :]
     sent(s1, 0)
     sent(s2, 1)
     sent(s3, 2)
     sent(s4, 3)
-    sent(ws, 4)
-    view = gr.at[pl.ds(0, chips - 1)]
-    pltpu.make_async_copy(view, view, send_sem.at[5]).wait()
+    drain(w1, mid1b, full1, 0)
+    pltpu.make_async_copy(full2, full2, line_recv.at[5]).wait()
+    for e in range(2):
+        proj_out[:, e * width : (e + 1) * width] = full2[e * width : (e + 1) * width, :]
+    drain(w2, mid2b, full2, 3)
 
 
 def local(
@@ -427,6 +465,9 @@
     hidden = out_weight.shape[0]
     count = rows * length
     parts = length // LANES
+    side = math.isqrt(chips)
+    share = 2 * side
+    block = 2 * width // share
     vm = pl.BlockSpec(memory_space=pltpu.VMEM)
     sm = pl.BlockSpec(memory_space=pltpu.SMEM)
     V = pltpu.VMEM
@@ -471,31 +512,33 @@
             V(eight, BF16),
             V((parts, rows * chips, LANES), F32),
             V((parts, rows * chips, LANES), F32),
-            V((4 * width, width), F32),
-            V((4 * chips, width), F32),
-            V((chips, 4, width), F32),
-            V((chips, 4, width), F32),
-            V((4, width), F32),
-            V((chips, 4, width), F32),
-            V((4 * chips, width), F32),
-            V((4 * chips, width), F32),
+            *(2 * [
+                V((2 * width, width), BF16),
+                V((share, block, width), BF16),
+                V((block, width), F32),
+                V((side, block, width), F32),
+                V((block, width), F32),
+                V((2 * width, width), F32),
+            ]),
+            pltpu.SemaphoreType.DMA((4,)),
+            pltpu.SemaphoreType.DMA((4,)),
+            pltpu.SemaphoreType.DMA((2,)),
+            pltpu.SemaphoreType.DMA((2,)),
             pltpu.SemaphoreType.DMA((6,)),
             pltpu.SemaphoreType.DMA((6,)),
-            pltpu.SemaphoreType.DMA((4,)),
-            pltpu.SemaphoreType.DMA((4,)),
         ],
         compiler_params=pltpu.CompilerParams(
-            collective_id=0, has_side_effects=True, vmem_limit_bytes=60 * 1024 * 1024
+            collective_id=0, has_side_effects=True, vmem_limit_bytes=20 * 1024 * 1024
         ),
     )(
         pair_act.reshape(count, width),
         out_grad.reshape(count, width),
-        pair_mask.reshape(rows, 1, length),
-        chain_ids.reshape(1, length),
+        pair_mask,
+        chain_ids,
         chain_ids,
         proj_weight,
         gate_weight,
-        chain_bias.T,
+        chain_bias,
         out_weight,
     )
     return (out[0].reshape(rows, length, width), out[1], out[2], out[3])

time: 104 us -> 95.5 us (0.918)
  Pallas kernels: 95.7 us -> 86.2 us
    pallas_call x1, Pallas kernels: 95.7 us -> 86.2 us  [local(): pl.pallas_call(kernel, out_shape=(jax.ShapeDtypeStruct((count, width), BF...]
    unnamed x15 -> x20, local copies, waits for them, and re-layouts: 5.39 us -> 8.22 us
    reshape x2 -> x0, local copies, waits for them, and re-layouts: 1.86 us -> none  [the longest x1 1.3 us: local(): pair_mask.reshape(rows, 1, length)]
where the time goes in v2:
time: 95.5 us; the launch traced here: 95.1 us
  Pallas kernels  86.2 us (90%)
  local copies, waits for them, and re-layouts  8.22 us (9%)
    pallas_call x1, Pallas kernels, local(): pl.pallas_call(kernel, out_shape=(jax.ShapeDtypeStruct((count, width), BF...  86.2 us
    unnamed x20, local copies, waits for them, and re-layouts  8.22 us

profile of v2, /device:TPU:513, one launch (start us, length us, event | category | flops | bytes accessed | tf_op | source)
XLA Modules:
  0.0 95.1 jit_solution(15190964376000605508)
XLA Ops:
  0.6 0.0 copy-start.5
  0.6 0.0 copy-start.7
  0.7 0.7 copy-done.5
  1.3 0.0 copy-done.7
  1.3 0.0 copy-start
  1.3 1.0 %copy-done = bf16[3,384,128]{2,1,0:T(8,128)(2,1)S(1)} copy-done((bf16[3,384,128]{2,1,0:T(8,128)(2,1)S(1)}, bf16[3,384,128]{2,1,0:T(8,128)(2,1)}, u32[]{:S(2)}) %copy-start) | copy-done | bytes 294936
  2.3 0.0 copy-start.1
  2.3 1.0 %copy-done.1 = bf16[3,384,128]{2,1,0:T(8,128)(2,1)S(1)} copy-done((bf16[3,384,128]{2,1,0:T(8,128)(2,1)S(1)}, bf16[3,384,128]{2,1,0:T(8,128)(2,1)}, u32[]{:S(2)}) %copy-start.1) | copy-done | bytes 294936
  3.3 0.0 copy-start.2
  3.3 0.8 copy-done.2
  4.1 0.0 copy-start.3
  4.1 0.8 copy-done.3
  4.9 0.0 copy-start.4
  4.9 0.7 copy-done.4
  5.6 0.0 copy-start.6
  5.6 0.7 copy-done.6
  6.3 86.2 %shard_map.111 = (bf16[1152,128]{1,0:T(8,128)(2,1)S(1)}, f32[128,256]{1,0:T(8,128)S(1)}, f32[128,128]{1,0:T(8,128)S(1)}, f32[64,128]{1,0:T(8,128)S(1)}) custom-call(bf16[1152,128]{1,0:T(8,128)(2,1)S(1)} %bitcast.3, bf16[1152,128]{1,0:T(8,128)(2,1)S(1)} %bitcast.4, s32[3,384]{1,0:T(4,128)S(1)} %copy-done.6, s32[384]{0:T(512)S(1)} %copy-done.5, ...), custom_call_target="tpu_custom_call" | custom-call | tf_op jit(solution)/shard_map/pallas_call | solution.py:475
  92.5 0.7 copy.16
  93.2 0.7 copy.17
  93.9 0.6 copy.18
  94.5 0.6 copy.19
Async XLA Ops:
  0.6 0.7 copy-start.5
  0.6 0.7 copy-start.7
  1.3 1.0 %copy-start = (bf16[3,384,128]{2,1,0:T(8,128)(2,1)S(1)}, bf16[3,384,128]{2,1,0:T(8,128)(2,1)}, u32[]{:S(2)}) copy-start(bf16[3,384,128]{2,1,0:T(8,128)(2,1)} %param.8) | copy-start | bytes 884740
  2.3 1.0 %copy-start.1 = (bf16[3,384,128]{2,1,0:T(8,128)(2,1)S(1)}, bf16[3,384,128]{2,1,0:T(8,128)(2,1)}, u32[]{:S(2)}) copy-start(bf16[3,384,128]{2,1,0:T(8,128)(2,1)} %param.15) | copy-start | bytes 884740
  3.3 0.8 copy-start.2
  4.1 0.8 copy-start.3
  4.9 0.7 copy-start.4
  5.6 0.7 copy-start.6

commit v3 on v2

--- a/solution.py
+++ b/solution.py
@@ -30,6 +30,18 @@
 
 
 def kernel(
+    act_hbm,
+    grad_hbm,
+    mask_hbm,
+    chain_hbm,
+    proj_hbm,
+    gate_hbm,
+    bias_hbm,
+    outw_hbm,
+    pair_out,
+    proj_out,
+    gate_out,
+    out_out,
     act_ref,
     grad_ref,
     mask_ref,
@@ -39,10 +51,7 @@
     gate_ref,
     bias_ref,
     outw_ref,
-    pair_out,
-    proj_out,
-    gate_out,
-    out_out,
+    in_sem,
     zhat_s,
     zscale_s,
     norm_s,
@@ -61,15 +70,20 @@
     a_s,
     b_s,
     dt_s,
-    s1,
-    r1,
+    spread2,
+    s1a,
+    s1b,
+    s2,
+    s3,
+    s4a,
+    s4b,
+    r1a,
+    r1b,
     r1p,
-    s2,
     r2,
-    s3,
     r3,
-    s4,
-    r4,
+    r4a,
+    r4b,
     half_s,
     half_r,
     w1,
@@ -84,6 +98,12 @@
     column2,
     mid2b,
     full2,
+    w3,
+    line3,
+    mid3a,
+    column3,
+    mid3b,
+    full3,
     send_sem,
     recv_sem,
     pair_send,
@@ -91,6 +111,24 @@
     line_send,
     line_recv,
 ):
+    loads = [
+        pltpu.make_async_copy(src, dst, in_sem.at[k])
+        for k, (src, dst) in enumerate(
+            (
+                (act_hbm, act_ref),
+                (proj_hbm, proj_ref),
+                (mask_hbm, mask_ref),
+                (grad_hbm, grad_ref),
+                (gate_hbm, gate_ref),
+                (outw_hbm, outw_ref),
+                (bias_hbm, bias_ref),
+                (chain_hbm, chain_ref),
+                (chain_hbm, own_ref),
+            )
+        )
+    ]
+    for load in loads:
+        load.start()
     me = lax.axis_index("cells")
     devices = lax.axis_size("cells")
     chips = devices // 2
@@ -104,7 +142,6 @@
     width = act_ref.shape[1]
     hidden = outw_ref.shape[0]
     parts = length // LANES
-    chunks = rows * parts
     tall = hidden // 8
     groups = chips // 8
 
@@ -189,10 +226,10 @@
 
         loop(chips, one, unroll=4)
 
-    def pack_rows(src, dst, at):
+    def pack_rows(src, dst):
         def one(t):
             for kq in range(parts):
-                dst[t, at : at + 4, kq * LANES : (kq + 1) * LANES] = src[
+                dst[t, :, kq * LANES : (kq + 1) * LANES] = src[
                     kq, pl.ds(t, 4, stride=chips), :
                 ].astype(BF16)
 
@@ -213,6 +250,9 @@
         lax.broadcasted_iota(jnp.int32, (width, width), 0)
         == lax.broadcasted_iota(jnp.int32, (width, width), 1)
     ).astype(BF16)
+
+    for load in loads[:3]:
+        load.wait()
 
     def front(r, kq):
         q = cols(kq, r)
@@ -235,13 +275,17 @@
         for ab in range(2):
             for g in range(tall):
                 at = ab * hidden + g * 8
-                spread[kq, pl.ds(g * 64 + ab * 4 + r, 8, stride=8), :] = factors[at : at + 8]
+                (spread, spread2)[ab][kq, pl.ds(g * 64 + r, 8, stride=8), :] = factors[at : at + 8]
 
     cells(front, unroll=3)
-    pack(spread, s1)
+    pack(spread2, s1b)
+    pack(spread, s1a)
     pl.semaphore_wait(barrier, chips + side - 1)
-    exchange(s1, r1, 0)
-
+    exchange(s1b, r1b, 0)
+    exchange(s1a, r1a, 1)
+
+    for load in loads[3:]:
+        load.wait()
     within, across = (
         jnp.sum(eye.astype(F32) * bias_ref[e : e + 1, :], axis=1, keepdims=True) for e in range(2)
     )
@@ -259,33 +303,35 @@
 
     cells(gating, unroll=3)
 
-    arrive(r1, 0)
-    first = to_partner(r1, r1p, 0)
-    unpack(r1, spread)
-    gather_rows(spread, 0, a_s)
+    arrive(r1b, 0)
+    first = to_partner(r1b, r1p, 0)
+    unpack(r1b, spread2)
 
     def place_right(src, which):
         for r in range(rows):
             for g in range(groups):
                 for kq in range(parts):
                     wide[kq, pl.ds(g * 48 + 3 * which + r, 8, stride=6), :] = src[
-                        kq, pl.ds(g * 64 + 4 + r, 8, stride=8), :
+                        kq, pl.ds(g * 64 + r, 8, stride=8), :
                     ]
 
-    place_right(spread, core)
+    place_right(spread2, core)
     first.wait()
-    unpack(r1p, spread)
-    place_right(spread, 1 - core)
+    unpack(r1p, spread2)
+    place_right(spread2, 1 - core)
+    arrive(r1a, 1)
+    unpack(r1a, spread)
+    gather_rows(spread, 0, a_s)
     for kq in range(parts):
         b_s[:, kq * LANES : (kq + 1) * LANES] = wide[kq].astype(BF16)
     for kq in range(parts):
         flat[kq, : rows * chips, :] = dot(
             a_s[...], b_s[kq * LANES : (kq + 1) * LANES, :], NT
         )
-    pack_rows(flat, s2, 0)
-    exchange(s2, r2, 1)
-
-    arrive(r2, 1)
+    pack_rows(flat, s2)
+    exchange(s2, r2, 2)
+
+    arrive(r2, 2)
     unpack(r2, spread)
 
     def middle(r, kq):
@@ -305,24 +351,20 @@
         m2 = jnp.mean(d_hat * hat, axis=0, keepdims=True)
         d_tri = scale * (d_hat - m1 - hat * m2)
         for g in range(tall):
-            spread[kq, pl.ds(g * 64 + 4 + r, 8, stride=8), :] = d_tri[g * 8 : g * 8 + 8]
+            spread2[kq, pl.ds(g * 64 + r, 8, stride=8), :] = d_tri[g * 8 : g * 8 + 8]
 
     cells(middle, unroll=3)
 
-    def pack_upper(t):
-        at = pl.ds(pl.multiple_of(t * 8, 8), 8)
-        for kq in range(parts):
-            s3[t, :, kq * LANES : (kq + 1) * LANES] = spread[kq, at, :][4:8].astype(BF16)
-
-    loop(chips, pack_upper, unroll=4)
-    exchange(s3, r3, 2)
+    pack(spread2, s3)
+    exchange(s3, r3, 3)
 
     share = 2 * side
     spot = col * 2 + core
-    block = w1.shape[0] // share
-
-    def own(m):
-        return pl.ds(pl.multiple_of(m * block, block), block)
+
+    def put(w, value):
+        n = w.shape[1]
+        for m in range(share):
+            w[m] = value[m * n : (m + 1) * n].astype(BF16)
 
     def line_peers(fn):
         for d in far:
@@ -341,8 +383,8 @@
         ).start()
 
     def scatter_line(src, dst, k):
-        line_peers(lambda p: send(src.at[own(lax.rem(p, share))], dst.at[spot], k, p))
-        pltpu.make_async_copy(src.at[own(spot)], dst.at[spot], line_recv.at[k]).start()
+        line_peers(lambda p: send(src.at[lax.rem(p, share)], dst.at[spot], k, p))
+        pltpu.make_async_copy(src.at[spot], dst.at[spot], line_recv.at[k]).start()
 
     def reduce_column(src, mid, dst, k):
         pltpu.make_async_copy(src, src, line_recv.at[k - 1]).wait()
@@ -354,21 +396,26 @@
 
     def gather_line(src, mid, dst, k):
         pltpu.make_async_copy(src, src, line_recv.at[k - 1]).wait()
-        mid[...] = jnp.sum(src[...], axis=0) * (1.0 / length)
-        line_peers(lambda p: send(mid, dst.at[own(spot)], k, p))
-        pltpu.make_async_copy(mid, dst.at[own(spot)], line_recv.at[k]).start()
-
-    def drain(w, mid, dst, k):
-        view = w.at[pl.ds(0, (share - 1) * block)]
-        pltpu.make_async_copy(view, view, line_send.at[k]).wait()
-        view = dst.at[pl.ds(0, (side - 1) * block)]
-        pltpu.make_async_copy(view, view, line_send.at[k + 1]).wait()
-        view = dst.at[pl.ds(0, (share - 1) * block)]
-        pltpu.make_async_copy(view, view, line_send.at[k + 2]).wait()
-
-    w1[0:width, :] = dot(norm_s[...], dl_s[...], NT).astype(BF16)
-    w1[width : width + hidden, :] = dot(trilow_s[...], do_s[...], NT).astype(BF16)
-    w1[width + hidden : 2 * width, :] = jnp.zeros((width - hidden, width), BF16)
+        mid[...] = (jnp.sum(src[...], axis=0) * (1.0 / length)).astype(BF16)
+        line_peers(lambda p: send(mid, dst.at[spot], k, p))
+        pltpu.make_async_copy(mid, dst.at[spot], line_recv.at[k]).start()
+
+    def drain(w, column, full, k):
+        for e, (src, n) in enumerate(((w, share), (column, side), (full, share))):
+            view = src.at[pl.ds(0, n - 1)]
+            pltpu.make_async_copy(view, view, line_send.at[k + e]).wait()
+
+    put(
+        w1,
+        jnp.concatenate(
+            [
+                dot(norm_s[...], dl_s[...], NT),
+                dot(trilow_s[...], do_s[...], NT),
+                jnp.zeros((width - hidden, width), F32),
+            ],
+            axis=0,
+        ),
+    )
     scatter_line(w1, line1, 0)
 
     def gate_part(r, kq):
@@ -377,7 +424,7 @@
 
     cells(gate_part, unroll=3)
 
-    arrive(r3, 2)
+    arrive(r3, 3)
     unpack(r3, spread)
     gather_rows(spread, 0, dt_s)
     for kq in range(parts):
@@ -393,7 +440,8 @@
         flat[kq, : rows * chips, :] = dot(
             dt_s[...], b_s[:, kq * LANES : (kq + 1) * LANES], NN
         )
-    pack_rows(flat, s4, 0)
+    pack_rows(flat, s4a)
+    exchange(s4a, r4a, 4)
     second.wait()
     for r in range(rows):
         for g in range(groups):
@@ -402,33 +450,34 @@
                 flat[kq, at, :] = (
                     wide[kq, pl.ds(g * 48 + 3 * core + r, 8, stride=6), :] + half_r[kq, at, :]
                 )
-    pack_rows(flat, s4, 4)
-    exchange(s4, r4, 3)
+    pack_rows(flat, s4b)
+    exchange(s4b, r4b, 5)
     reduce_column(line1, mid1a, column1, 1)
 
-    arrive(r4, 3)
-    unpack(r4, spread)
-
-    def factor_back(r, kq):
-        q = cols(kq, r)
-        d_factors = jnp.concatenate(
-            [
-                spread[kq, pl.ds(g * 64 + ab * 4 + r, 8, stride=8), :]
-                for ab in range(2)
-                for g in range(tall)
-            ],
-            axis=0,
-        )
-        dproj_s[: 2 * hidden, q] = (d_factors * p1_s[:, q]).astype(BF16)
-        dproj_s[2 * hidden :, q] = (d_factors * p2_s[:, q]).astype(BF16)
-
-    cells(factor_back, unroll=3)
-    for e in range(2):
-        w2[e * width : (e + 1) * width, :] = dot(
-            norm_s[...], dproj_s[e * width : (e + 1) * width, :], NT
-        ).astype(BF16)
-    scatter_line(w2, line2, 3)
+    def half_back(ab, src, k, w, line, base):
+        arrive(src, k)
+        unpack(src, spread)
+        at = slice(ab * hidden, (ab + 1) * hidden)
+        up = slice((2 + ab) * hidden, (3 + ab) * hidden)
+
+        def factor_back(r, kq):
+            q = cols(kq, r)
+            d_factors = jnp.concatenate(
+                [spread[kq, pl.ds(g * 64 + r, 8, stride=8), :] for g in range(tall)], axis=0
+            )
+            dproj_s[at, q] = (d_factors * p1_s[at, q]).astype(BF16)
+            dproj_s[up, q] = (d_factors * p2_s[at, q]).astype(BF16)
+
+        cells(factor_back, unroll=3)
+        put(
+            w,
+            dot(norm_s[...], jnp.concatenate([dproj_s[at, :], dproj_s[up, :]], axis=0), NT),
+        )
+        scatter_line(w, line, base)
+
+    half_back(0, r4a, 4, w2, line2, 3)
     gather_line(column1, mid1b, full1, 2)
+    half_back(1, r4b, 5, w3, line3, 6)
 
     def finish(r, kq):
         q = cols(kq, r)
@@ -439,21 +488,41 @@
         grad = zscale_s[:, q] * (d_norm - m1 - zhat * m2)
         pair_out[q, :] = grad.T.astype(BF16)
 
+    reduce_column(line2, mid2a, column2, 4)
     cells(finish, unroll=3)
-    reduce_column(line2, mid2a, column2, 4)
+    reduce_column(line3, mid3a, column3, 7)
     gather_line(column2, mid2b, full2, 5)
-    pltpu.make_async_copy(full1, full1, line_recv.at[2]).wait()
-    gate_out[...] = full1[0:width, :]
-    out_out[...] = full1[width : width + hidden, :]
-    sent(s1, 0)
-    sent(s2, 1)
-    sent(s3, 2)
-    sent(s4, 3)
-    drain(w1, mid1b, full1, 0)
-    pltpu.make_async_copy(full2, full2, line_recv.at[5]).wait()
-    for e in range(2):
-        proj_out[:, e * width : (e + 1) * width] = full2[e * width : (e + 1) * width, :]
-    drain(w2, mid2b, full2, 3)
+
+    def landed(full, k):
+        pltpu.make_async_copy(full, full, line_recv.at[k]).wait()
+        return full[...].astype(F32).reshape(full.shape[0] * full.shape[1], width)
+
+    gather_line(column3, mid3b, full3, 8)
+    sums = landed(full1, 2)
+    gate_out[...] = sums[0:width]
+    out_out[...] = sums[width : width + hidden]
+    for k, src in enumerate((s1b, s1a, s2, s3, s4a, s4b)):
+        sent(src, k)
+    drain(w1, column1, full1, 0)
+    drain(w2, column2, full2, 3)
+    left, right = landed(full2, 5), landed(full3, 8)
+    lower = lax.broadcasted_iota(jnp.int32, left.shape, 1) < hidden
+    proj_out[:, 0:width] = jnp.where(lower, left, pltpu.roll(right, hidden, 1))
+    proj_out[:, width : 2 * width] = jnp.where(lower, pltpu.roll(left, hidden, 1), right)
+    drain(w3, column3, full3, 6)
+
+
+def write(a_ref, b_ref, c_ref, d_ref, a_out, b_out, c_out, d_out, sem):
+    copies = [
+        pltpu.make_async_copy(src, dst, sem.at[k])
+        for k, (src, dst) in enumerate(
+            ((a_ref, a_out), (b_ref, b_out), (c_ref, c_out), (d_ref, d_out))
+        )
+    ]
+    for copy in copies:
+        copy.start()
+    for copy in copies:
+        copy.wait()
 
 
 def local(
@@ -467,22 +536,43 @@
     parts = length // LANES
     side = math.isqrt(chips)
     share = 2 * side
-    block = 2 * width // share
     vm = pl.BlockSpec(memory_space=pltpu.VMEM)
-    sm = pl.BlockSpec(memory_space=pltpu.SMEM)
+    hbm = pl.BlockSpec(memory_space=pltpu.HBM)
     V = pltpu.VMEM
-    eight, four = (chips, 8, length), (chips, 4, length)
+    four = (chips, 4, length)
+
+    def reduction(block):
+        return [
+            V((share, block, width), BF16),
+            V((share, block, width), BF16),
+            V((block, width), F32),
+            V((side, block, width), F32),
+            V((block, width), BF16),
+            V((share, block, width), BF16),
+        ]
+
+    shapes = (
+        jax.ShapeDtypeStruct((count, width), BF16),
+        jax.ShapeDtypeStruct((width, 4 * hidden), F32),
+        jax.ShapeDtypeStruct((width, width), F32),
+        jax.ShapeDtypeStruct((hidden, width), F32),
+    )
     out = pl.pallas_call(
         kernel,
-        out_shape=(
-            jax.ShapeDtypeStruct((count, width), BF16),
-            jax.ShapeDtypeStruct((width, 4 * hidden), F32),
-            jax.ShapeDtypeStruct((width, width), F32),
-            jax.ShapeDtypeStruct((hidden, width), F32),
-        ),
-        in_specs=[vm, vm, vm, vm, sm, vm, vm, vm, vm],
+        out_shape=shapes,
+        in_specs=8 * [hbm],
         out_specs=(vm, vm, vm, vm),
         scratch_shapes=[
+            V((count, width), BF16),
+            V((count, width), BF16),
+            V((rows, length), jnp.int32),
+            V((length,), jnp.int32),
+            pltpu.SMEM((length,), jnp.int32),
+            V((width, 4 * hidden), BF16),
+            V((width, width), BF16),
+            V((2, width), F32),
+            V((hidden, width), BF16),
+            pltpu.SemaphoreType.DMA((9,)),
             V((width, count), F32),
             V((1, count), F32),
             V((width, count), BF16),
@@ -501,46 +591,46 @@
             V((rows * chips, length), BF16),
             V((length, length), BF16),
             V((rows * chips, length), BF16),
-            V(eight, BF16),
-            V(eight, BF16),
-            V(eight, BF16),
-            V(four, BF16),
-            V(four, BF16),
-            V(four, BF16),
-            V(four, BF16),
-            V(eight, BF16),
-            V(eight, BF16),
+            V((parts, 8 * chips, LANES), F32),
+            *(13 * [V(four, BF16)]),
             V((parts, rows * chips, LANES), F32),
             V((parts, rows * chips, LANES), F32),
-            *(2 * [
-                V((2 * width, width), BF16),
-                V((share, block, width), BF16),
-                V((block, width), F32),
-                V((side, block, width), F32),
-                V((block, width), F32),
-                V((2 * width, width), F32),
-            ]),
-            pltpu.SemaphoreType.DMA((4,)),
-            pltpu.SemaphoreType.DMA((4,)),
+            *reduction(2 * width // share),
+            *reduction(width // share),
+            *reduction(width // share),
+            pltpu.SemaphoreType.DMA((6,)),
+            pltpu.SemaphoreType.DMA((6,)),
             pltpu.SemaphoreType.DMA((2,)),
             pltpu.SemaphoreType.DMA((2,)),
-            pltpu.SemaphoreType.DMA((6,)),
-            pltpu.SemaphoreType.DMA((6,)),
+            pltpu.SemaphoreType.DMA((9,)),
+            pltpu.SemaphoreType.DMA((9,)),
         ],
         compiler_params=pltpu.CompilerParams(
             collective_id=0, has_side_effects=True, vmem_limit_bytes=20 * 1024 * 1024
         ),
     )(
-        pair_act.reshape(count, width),
-        out_grad.reshape(count, width),
-        pair_mask,
-        chain_ids,
-        chain_ids,
-        proj_weight,
-        gate_weight,
-        chain_bias,
-        out_weight,
+        *(
+            pltpu.with_memory_space_constraint(x, pltpu.HBM)
+            for x in (
+                pair_act.reshape(count, width),
+                out_grad.reshape(count, width),
+                pair_mask,
+                chain_ids,
+                proj_weight,
+                gate_weight,
+                chain_bias,
+                out_weight,
+            )
+        )
     )
+    out = pl.pallas_call(
+        write,
+        out_shape=shapes,
+        in_specs=4 * [vm],
+        out_specs=tuple(4 * [hbm]),
+        scratch_shapes=[pltpu.SemaphoreType.DMA((4,))],
+        compiler_params=pltpu.CompilerParams(vmem_limit_bytes=4 * 1024 * 1024),
+    )(*out)
     return (out[0].reshape(rows, length, width), out[1], out[2], out[3])
 
 

time: 95.5 us -> 82 us (0.86)
  local copies, waits for them, and re-layouts: 8.22 us -> 0 us
  Pallas kernels: 86.2 us -> 81.2 us
    unnamed x20 -> x0, local copies, waits for them, and re-layouts: 8.22 us -> none
    pallas_call x1 -> x2, Pallas kernels: 86.2 us -> 81.2 us  [the longest x1 80.4 us: local(): pl.pallas_call(kernel, out_shape=shapes, in_specs=8 * [hbm], out_specs=(v...]
where the time goes in v3:
time: 82 us; the launch traced here: 81.9 us
  Pallas kernels  81.2 us (99%)
    pallas_call x1, Pallas kernels, local(): pl.pallas_call(kernel, out_shape=shapes, in_specs=8 * [hbm], out_specs=(v...  80.4 us

profile of v3, /device:TPU:513, one launch (start us, length us, event | category | flops | bytes accessed | tf_op | source)
XLA Modules:
  0.0 81.9 jit_solution(3033493480198614990)
XLA Ops:
  0.6 80.4 %shard_map.111 = (bf16[1152,128]{1,0:T(8,128)(2,1)S(1)}, f32[128,256]{1,0:T(8,128)S(1)}, f32[128,128]{1,0:T(8,128)S(1)}, f32[64,128]{1,0:T(8,128)S(1)}) custom-call(bf16[1152,128]{1,0:T(8,128)(2,1)} %bitcast.3, bf16[1152,128]{1,0:T(8,128)(2,1)} %bitcast.4, s32[3,384]{1,0:T(4,128)} %mask_hbm.1, s32[384]{0:T(512)} %chain_hbm.1, bf16[128,256]{1,0:T(8,128)(2,1)} %proj_hbm.1, ...), custom_call_target="tpu_custom_call" | custom-call | tf_op jit(solution)/shard_map/pallas_call | solution.py:560
  81.1 0.8 shard_map.112

commit v4 on v3

--- a/solution.py
+++ b/solution.py
@@ -12,6 +12,7 @@
 F32 = jnp.float32
 BF16 = jnp.bfloat16
 LANES = 128
+SLOT = 24
 NT = (((1,), (1,)), ((), ()))
 TN = (((0,), (0,)), ((), ()))
 NN = (((1,), (0,)), ((), ()))
@@ -144,16 +145,25 @@
     parts = length // LANES
     tall = hidden // 8
     groups = chips // 8
+    pairs = (rows * parts + 1) // 2
 
     barrier = pltpu.get_barrier_semaphore()
 
-    def each_chip(fn):
+    def base_of(i):
+        step = side // 2 + ((i + 1) // 2) * (1 - 2 * lax.rem(i, 2))
+        return lax.rem(row + step, side) * side
+
+    def each_chip(fn, prepare=None):
         def line(i):
-            step = side // 2 + ((i + 1) // 2) * (1 - 2 * lax.rem(i, 2))
-            base = lax.rem(row + step, side) * side
-            for d in far:
+            base, later = base_of(i), base_of(i + 1)
+            for k, d in enumerate(far):
+                if prepare is not None:
+                    prepare(later + k)
                 fn(base + lax.rem(col + d, side))
 
+        if prepare is not None:
+            for k in range(side):
+                prepare(base_of(jnp.int32(0)) + k)
         loop(side - 1, line)
         for d in far[:-1]:
             fn(row * side + lax.rem(col + d, side))
@@ -166,7 +176,7 @@
         greet((row * side + lax.rem(col + d, side)) * 2 + 1 - core)
     greet(partner)
 
-    def exchange(src, dst, k):
+    def exchange(src, dst, k, prepare=None):
         def one(t):
             pltpu.make_async_remote_copy(
                 src_ref=src.at[t],
@@ -177,7 +187,7 @@
                 device_id_type=MESH,
             ).start()
 
-        each_chip(one)
+        each_chip(one, prepare)
         pltpu.make_async_copy(src.at[chip], dst.at[chip], recv_sem.at[k]).start()
 
     def arrive(dst, k):
@@ -207,44 +217,38 @@
             loop(parts, lambda kq, r=r: body(r, kq), unroll)
 
     def unpack(src, dst):
-        n = src.shape[1]
-
         def one(t):
-            at = pl.ds(pl.multiple_of(t * 8, 8), n)
-            for kq in range(parts):
-                dst[kq, at, :] = src[t, :, kq * LANES : (kq + 1) * LANES].astype(F32)
+            for i in range(pairs):
+                dst[pl.ds(pl.multiple_of(t * SLOT, 8) + 2 * i, 2), :] = src[t, i].astype(F32)
 
         loop(chips, one, unroll=4)
 
     def pack(src, dst):
-        n = dst.shape[1]
-
         def one(t):
-            at = pl.ds(pl.multiple_of(t * 8, 8), n)
-            for kq in range(parts):
-                dst[t, :, kq * LANES : (kq + 1) * LANES] = src[kq, at, :].astype(BF16)
-
-        loop(chips, one, unroll=4)
+            for i in range(pairs):
+                at = pl.ds(pl.multiple_of(t * SLOT, 8) + 2 * i, 2)
+                dst[t, i] = src[at, :].astype(BF16)
+
+        return one
 
     def pack_rows(src, dst):
         def one(t):
-            for kq in range(parts):
-                dst[t, :, kq * LANES : (kq + 1) * LANES] = src[
-                    kq, pl.ds(t, 4, stride=chips), :
-                ].astype(BF16)
-
-        loop(chips, one, unroll=4)
-
-    def gather_rows(src, offset, dst):
+            for i in range(pairs):
+                dst[t, i] = src[pl.ds(2 * i * chips + t, 2, stride=chips), :].astype(BF16)
+
+        return one
+
+    def eight(src, g, r, kq):
+        return src[pl.ds(g * 8 * SLOT + r * parts + kq, 8, stride=SLOT), :]
+
+    def gather_rows(src, dst):
         for r in range(rows):
             for g in range(0, groups, 2):
+                at = r * chips + g * 8
                 for kq in range(parts):
-                    both = [
-                        src[kq, pl.ds((g + e) * 64 + offset + r, 8, stride=8), :] for e in range(2)
-                    ]
-                    dst[
-                        r * chips + g * 8 : r * chips + g * 8 + 16, kq * LANES : (kq + 1) * LANES
-                    ] = jnp.concatenate(both, axis=0).astype(BF16)
+                    dst[at : at + 16, kq * LANES : (kq + 1) * LANES] = jnp.concatenate(
+                        [eight(src, g, r, kq), eight(src, g + 1, r, kq)], axis=0
+                    ).astype(BF16)
 
     eye = (
         lax.broadcasted_iota(jnp.int32, (width, width), 0)
@@ -275,11 +279,13 @@
         for ab in range(2):
             for g in range(tall):
                 at = ab * hidden + g * 8
-                (spread, spread2)[ab][kq, pl.ds(g * 64 + r, 8, stride=8), :] = factors[at : at + 8]
+                (spread, spread2)[ab][
+                    pl.ds(g * 8 * SLOT + r * parts + kq, 8, stride=SLOT), :
+                ] = factors[at : at + 8]
 
     cells(front, unroll=3)
-    pack(spread2, s1b)
-    pack(spread, s1a)
+    loop(chips, pack(spread2, s1b), unroll=4)
+    loop(chips, pack(spread, s1a), unroll=4)
     pl.semaphore_wait(barrier, chips + side - 1)
     exchange(s1b, r1b, 0)
     exchange(s1a, r1a, 1)
@@ -311,9 +317,7 @@
         for r in range(rows):
             for g in range(groups):
                 for kq in range(parts):
-                    wide[kq, pl.ds(g * 48 + 3 * which + r, 8, stride=6), :] = src[
-                        kq, pl.ds(g * 64 + r, 8, stride=8), :
-                    ]
+                    wide[kq, pl.ds(g * 48 + 3 * which + r, 8, stride=6), :] = eight(src, g, r, kq)
 
     place_right(spread2, core)
     first.wait()
@@ -321,15 +325,15 @@
     place_right(spread2, 1 - core)
     arrive(r1a, 1)
     unpack(r1a, spread)
-    gather_rows(spread, 0, a_s)
+    gather_rows(spread, a_s)
     for kq in range(parts):
         b_s[:, kq * LANES : (kq + 1) * LANES] = wide[kq].astype(BF16)
     for kq in range(parts):
-        flat[kq, : rows * chips, :] = dot(
-            a_s[...], b_s[kq * LANES : (kq + 1) * LANES, :], NT
-        )
-    pack_rows(flat, s2)
-    exchange(s2, r2, 2)
+        product = dot(a_s[...], b_s[kq * LANES : (kq + 1) * LANES, :], NT)
+        for r in range(rows):
+            at = (r * parts + kq) * chips
+            flat[at : at + chips, :] = product[r * chips : (r + 1) * chips]
+    exchange(s2, r2, 2, pack_rows(flat, s2))
 
     arrive(r2, 2)
     unpack(r2, spread)
@@ -337,7 +341,7 @@
     def middle(r, kq):
         q = cols(kq, r)
         tri = jnp.concatenate(
-            [spread[kq, pl.ds(g * 64 + r, 8, stride=8), :] for g in range(tall)], axis=0
+            [eight(spread, g, r, kq) for g in range(tall)], axis=0
         )
         center = tri - jnp.mean(tri, axis=0, keepdims=True)
         scale = lax.rsqrt(jnp.mean(center * center, axis=0, keepdims=True) + EPS)
@@ -351,12 +355,13 @@
         m2 = jnp.mean(d_hat * hat, axis=0, keepdims=True)
         d_tri = scale * (d_hat - m1 - hat * m2)
         for g in range(tall):
-            spread2[kq, pl.ds(g * 64 + r, 8, stride=8), :] = d_tri[g * 8 : g * 8 + 8]
+            spread2[pl.ds(g * 8 * SLOT + r * parts + kq, 8, stride=SLOT), :] = d_tri[
+                g * 8 : g * 8 + 8
+            ]
 
     cells(middle, unroll=3)
 
-    pack(spread2, s3)
-    exchange(s3, r3, 3)
+    exchange(s3, r3, 3, pack(spread2, s3))
 
     share = 2 * side
     spot = col * 2 + core
@@ -426,32 +431,32 @@
 
     arrive(r3, 3)
     unpack(r3, spread)
-    gather_rows(spread, 0, dt_s)
+    gather_rows(spread, dt_s)
+    second = []
     for kq in range(parts):
         wide[kq] = dot(dt_s[...], a_s[:, kq * LANES : (kq + 1) * LANES], TN)
-    for r in range(rows):
-        for g in range(groups):
-            for kq in range(parts):
+        for r in range(rows):
+            for g in range(groups):
                 half_s[kq, r * chips + g * 8 : r * chips + g * 8 + 8, :] = wide[
                     kq, pl.ds(g * 48 + 3 * (1 - core) + r, 8, stride=6), :
                 ]
-    second = to_partner(half_s, half_r, 1)
+        second.append(to_partner(half_s.at[kq], half_r.at[kq], 1 + kq))
     for kq in range(parts):
-        flat[kq, : rows * chips, :] = dot(
-            dt_s[...], b_s[:, kq * LANES : (kq + 1) * LANES], NN
-        )
-    pack_rows(flat, s4a)
-    exchange(s4a, r4a, 4)
-    second.wait()
-    for r in range(rows):
-        for g in range(groups):
-            for kq in range(parts):
-                at = slice(r * chips + g * 8, r * chips + g * 8 + 8)
-                flat[kq, at, :] = (
-                    wide[kq, pl.ds(g * 48 + 3 * core + r, 8, stride=6), :] + half_r[kq, at, :]
+        product = dot(dt_s[...], b_s[:, kq * LANES : (kq + 1) * LANES], NN)
+        for r in range(rows):
+            at = (r * parts + kq) * chips
+            flat[at : at + chips, :] = product[r * chips : (r + 1) * chips]
+    exchange(s4a, r4a, 4, pack_rows(flat, s4a))
+    for kq in range(parts):
+        second[kq].wait()
+        for r in range(rows):
+            for g in range(groups):
+                at = (r * parts + kq) * chips + g * 8
+                flat[at : at + 8, :] = (
+                    wide[kq, pl.ds(g * 48 + 3 * core + r, 8, stride=6), :]
+                    + half_r[kq, r * chips + g * 8 : r * chips + g * 8 + 8, :]
                 )
-    pack_rows(flat, s4b)
-    exchange(s4b, r4b, 5)
+    exchange(s4b, r4b, 5, pack_rows(flat, s4b))
     reduce_column(line1, mid1a, column1, 1)
 
     def half_back(ab, src, k, w, line, base):
@@ -463,7 +468,7 @@
         def factor_back(r, kq):
             q = cols(kq, r)
             d_factors = jnp.concatenate(
-                [spread[kq, pl.ds(g * 64 + r, 8, stride=8), :] for g in range(tall)], axis=0
+                [eight(spread, g, r, kq) for g in range(tall)], axis=0
             )
             dproj_s[at, q] = (d_factors * p1_s[at, q]).astype(BF16)
             dproj_s[up, q] = (d_factors * p2_s[at, q]).astype(BF16)
@@ -476,8 +481,8 @@
         scatter_line(w, line, base)
 
     half_back(0, r4a, 4, w2, line2, 3)
+    half_back(1, r4b, 5, w3, line3, 6)
     gather_line(column1, mid1b, full1, 2)
-    half_back(1, r4b, 5, w3, line3, 6)
 
     def finish(r, kq):
         q = cols(kq, r)
@@ -539,7 +544,8 @@
     vm = pl.BlockSpec(memory_space=pltpu.VMEM)
     hbm = pl.BlockSpec(memory_space=pltpu.HBM)
     V = pltpu.VMEM
-    four = (chips, 4, length)
+    pairs = (rows * parts + 1) // 2
+    slots = (chips, pairs, 2, LANES)
 
     def reduction(block):
         return [
@@ -585,14 +591,14 @@
             V((width, count), F32),
             V((hidden, count), BF16),
             V((4 * hidden, count), BF16),
-            V((parts, 8 * chips, LANES), F32),
+            V((SLOT * chips, LANES), F32),
             V((parts, length, LANES), F32),
-            V((parts, 4 * chips, LANES), F32),
+            V((2 * pairs * chips, LANES), F32),
             V((rows * chips, length), BF16),
             V((length, length), BF16),
             V((rows * chips, length), BF16),
-            V((parts, 8 * chips, LANES), F32),
-            *(13 * [V(four, BF16)]),
+            V((SLOT * chips, LANES), F32),
+            *(13 * [V(slots, BF16)]),
             V((parts, rows * chips, LANES), F32),
             V((parts, rows * chips, LANES), F32),
             *reduction(2 * width // share),
@@ -600,8 +606,8 @@
             *reduction(width // share),
             pltpu.SemaphoreType.DMA((6,)),
             pltpu.SemaphoreType.DMA((6,)),
-            pltpu.SemaphoreType.DMA((2,)),
-            pltpu.SemaphoreType.DMA((2,)),
+            pltpu.SemaphoreType.DMA((1 + parts,)),
+            pltpu.SemaphoreType.DMA((1 + parts,)),
             pltpu.SemaphoreType.DMA((9,)),
             pltpu.SemaphoreType.DMA((9,)),
         ],

time: 82 us -> 78.2 us (0.954)
  Pallas kernels: 81.2 us -> 77.5 us
    pallas_call x1, Pallas kernels: 80.4 us -> 76.7 us  [local(): pl.pallas_call(kernel, out_shape=shapes, in_specs=8 * [hbm], out_specs=(v...]
where the time goes in v4:
time: 78.2 us; the launch traced here: 78.1 us
  Pallas kernels  77.5 us (99%)
    pallas_call x1, Pallas kernels, local(): pl.pallas_call(kernel, out_shape=shapes, in_specs=8 * [hbm], out_specs=(v...  76.7 us

profile of v4, /device:TPU:513, one launch (start us, length us, event | category | flops | bytes accessed | tf_op | source)
XLA Modules:
  0.0 78.1 jit_solution(9424533732075702432)
XLA Ops:
  0.6 76.7 %shard_map.111 = (bf16[1152,128]{1,0:T(8,128)(2,1)S(1)}, f32[128,256]{1,0:T(8,128)S(1)}, f32[128,128]{1,0:T(8,128)S(1)}, f32[64,128]{1,0:T(8,128)S(1)}) custom-call(bf16[1152,128]{1,0:T(8,128)(2,1)} %bitcast.3, bf16[1152,128]{1,0:T(8,128)(2,1)} %bitcast.4, s32[3,384]{1,0:T(4,128)} %mask_hbm.1, s32[384]{0:T(512)} %chain_hbm.1, bf16[128,256]{1,0:T(8,128)(2,1)} %proj_hbm.1, ...), custom_call_target="tpu_custom_call" | custom-call | tf_op jit(solution)/shard_map/pallas_call | solution.py:566
  77.3 0.8 %shard_map.112 = (bf16[1152,128]{1,0:T(8,128)(2,1)}, f32[128,256]{1,0:T(8,128)}, f32[128,128]{1,0:T(8,128)}, f32[64,128]{1,0:T(8,128)}) custom-call(bf16[1152,128]{1,0:T(8,128)(2,1)S(1)} %get-tuple-element.12.a_ref, f32[128,256]{1,0:T(8,128)S(1)} %get-tuple-element.13.b_ref, f32[128,128]{1,0:T(8,128)S(1)} %get-tuple-element.14.c_ref, ...), custom_call_target="tpu_custom_call" | custom-call | tf_op jit(solution)/shard_map/pallas_call | solution.py:632

commit v5 on v4

--- a/solution.py
+++ b/solution.py
@@ -93,6 +93,9 @@
     column1,
     mid1b,
     full1,
+    few,
+    projt_s,
+    col_recv,
     w2,
     line2,
     mid2a,
@@ -176,19 +179,21 @@
         greet((row * side + lax.rem(col + d, side)) * 2 + 1 - core)
     greet(partner)
 
-    def exchange(src, dst, k, prepare=None):
+    def exchange(src, dst, k, prepare=None, recv=None):
+        recv = recv_sem.at[k] if recv is None else recv
+
         def one(t):
             pltpu.make_async_remote_copy(
                 src_ref=src.at[t],
                 dst_ref=dst.at[chip],
                 send_sem=send_sem.at[k],
-                recv_sem=recv_sem.at[k],
+                recv_sem=recv,
                 device_id={"cells": t * 2 + core},
                 device_id_type=MESH,
             ).start()
 
         each_chip(one, prepare)
-        pltpu.make_async_copy(src.at[chip], dst.at[chip], recv_sem.at[k]).start()
+        pltpu.make_async_copy(src.at[chip], dst.at[chip], recv).start()
 
     def arrive(dst, k):
         pltpu.make_async_copy(dst, dst, recv_sem.at[k]).wait()
@@ -216,17 +221,22 @@
         for r in range(rows):
             loop(parts, lambda kq, r=r: body(r, kq), unroll)
 
+    lead = side * SLOT + 8
+
+    def slot(t):
+        return pl.multiple_of(t * SLOT + t // side * 8, 8)
+
     def unpack(src, dst):
         def one(t):
             for i in range(pairs):
-                dst[pl.ds(pl.multiple_of(t * SLOT, 8) + 2 * i, 2), :] = src[t, i].astype(F32)
+                dst[pl.ds(slot(t) + 2 * i, 2), :] = src[t, i].astype(F32)
 
         loop(chips, one, unroll=4)
 
     def pack(src, dst):
         def one(t):
             for i in range(pairs):
-                at = pl.ds(pl.multiple_of(t * SLOT, 8) + 2 * i, 2)
+                at = pl.ds(slot(t) + 2 * i, 2)
                 dst[t, i] = src[at, :].astype(BF16)
 
         return one
@@ -239,7 +249,10 @@
         return one
 
     def eight(src, g, r, kq):
-        return src[pl.ds(g * 8 * SLOT + r * parts + kq, 8, stride=SLOT), :]
+        return src[pl.ds(g * lead + r * parts + kq, 8, stride=SLOT), :]
+
+    def channels(g, r, kq):
+        return pl.ds(g * SLOT + r * parts + kq, 8, stride=lead)
 
     def gather_rows(src, dst):
         for r in range(rows):
@@ -280,7 +293,7 @@
             for g in range(tall):
                 at = ab * hidden + g * 8
                 (spread, spread2)[ab][
-                    pl.ds(g * 8 * SLOT + r * parts + kq, 8, stride=SLOT), :
+                    channels(g, r, kq), :
                 ] = factors[at : at + 8]
 
     cells(front, unroll=3)
@@ -308,6 +321,15 @@
         dh_s[:, q] = dot(outw_ref[...], low, NN)
 
     cells(gating, unroll=3)
+    flipped = proj_ref[...].astype(F32).T
+    for ab in range(2):
+        for x in range(side):
+            both = [
+                flipped[(2 * e + ab) * hidden + x * 8 : (2 * e + ab) * hidden + x * 8 + 8]
+                for e in range(2)
+            ]
+            at = 2 * (ab * hidden + x * 8)
+            projt_s[at : at + 16, :] = jnp.concatenate(both, axis=0).astype(BF16)
 
     arrive(r1b, 0)
     first = to_partner(r1b, r1p, 0)
@@ -341,7 +363,7 @@
     def middle(r, kq):
         q = cols(kq, r)
         tri = jnp.concatenate(
-            [eight(spread, g, r, kq) for g in range(tall)], axis=0
+            [spread[channels(g, r, kq), :] for g in range(tall)], axis=0
         )
         center = tri - jnp.mean(tri, axis=0, keepdims=True)
         scale = lax.rsqrt(jnp.mean(center * center, axis=0, keepdims=True) + EPS)
@@ -355,7 +377,7 @@
         m2 = jnp.mean(d_hat * hat, axis=0, keepdims=True)
         d_tri = scale * (d_hat - m1 - hat * m2)
         for g in range(tall):
-            spread2[pl.ds(g * 8 * SLOT + r * parts + kq, 8, stride=SLOT), :] = d_tri[
+            spread2[channels(g, r, kq), :] = d_tri[
                 g * 8 : g * 8 + 8
             ]
 
@@ -406,7 +428,7 @@
         pltpu.make_async_copy(mid, dst.at[spot], line_recv.at[k]).start()
 
     def drain(w, column, full, k):
-        for e, (src, n) in enumerate(((w, share), (column, side), (full, share))):
+        for e, (src, n) in enumerate(((full, share), (column, side), (full, share))):
             view = src.at[pl.ds(0, n - 1)]
             pltpu.make_async_copy(view, view, line_send.at[k + e]).wait()
 
@@ -446,7 +468,7 @@
         for r in range(rows):
             at = (r * parts + kq) * chips
             flat[at : at + chips, :] = product[r * chips : (r + 1) * chips]
-    exchange(s4a, r4a, 4, pack_rows(flat, s4a))
+    exchange(s4a, r4a, 4, pack_rows(flat, s4a), col_recv.at[0, col])
     for kq in range(parts):
         second[kq].wait()
         for r in range(rows):
@@ -456,37 +478,45 @@
                     wide[kq, pl.ds(g * 48 + 3 * core + r, 8, stride=6), :]
                     + half_r[kq, r * chips + g * 8 : r * chips + g * 8 + 8, :]
                 )
-    exchange(s4b, r4b, 5, pack_rows(flat, s4b))
+    exchange(s4b, r4b, 5, pack_rows(flat, s4b), col_recv.at[1, col])
     reduce_column(line1, mid1a, column1, 1)
 
-    def half_back(ab, src, k, w, line, base):
-        arrive(src, k)
-        unpack(src, spread)
-        at = slice(ab * hidden, (ab + 1) * hidden)
-        up = slice((2 + ab) * hidden, (3 + ab) * hidden)
-
-        def factor_back(r, kq):
-            q = cols(kq, r)
-            d_factors = jnp.concatenate(
-                [eight(spread, g, r, kq) for g in range(tall)], axis=0
-            )
-            dproj_s[at, q] = (d_factors * p1_s[at, q]).astype(BF16)
-            dproj_s[up, q] = (d_factors * p2_s[at, q]).astype(BF16)
-
-        cells(factor_back, unroll=3)
-        put(
-            w,
-            dot(norm_s[...], jnp.concatenate([dproj_s[at, :], dproj_s[up, :]], axis=0), NT),
-        )
-        scatter_line(w, line, base)
-
-    half_back(0, r4a, 4, w2, line2, 3)
-    half_back(1, r4b, 5, w3, line3, 6)
+    def half_back(ab, src, w, line, k):
+        for d in reversed(far):
+            x = lax.rem(col + d, side)
+            view = src.at[pl.ds(0, side)]
+            pltpu.make_async_copy(view, view, col_recv.at[ab, x]).wait()
+            for y in range(side):
+                for i in range(pairs):
+                    few[y * SLOT + 2 * i : y * SLOT + 2 * i + 2, :] = src[
+                        y * side + x, i
+                    ].astype(F32)
+            at = pl.ds(pl.multiple_of(ab * hidden + x * 8, 8), 8)
+            to = pl.ds(pl.multiple_of(2 * (ab * hidden + x * 8), 16), 16)
+            for r in range(rows):
+                for kq in range(parts):
+                    q = slice((r * parts + kq) * LANES, (r * parts + kq + 1) * LANES)
+                    d_factors = few[pl.ds(r * parts + kq, 8, stride=SLOT), :]
+                    both = [d_factors * p1_s[at, q], d_factors * p2_s[at, q]]
+                    dproj_s[to, q] = jnp.concatenate(both, axis=0).astype(BF16)
+            term = dot(dproj_s[to, :], norm_s[...], NT)
+            across_line = (row * side + lax.rem(x + side // 2, side)) * 2
+            for e in range(2):
+                w[x, e] = term[8 * e : 8 * e + 8].astype(BF16)
+            for e in range(2):
+                half = 1 - core if e else core
+                if e or d != side // 2:
+                    send(w.at[x, half], line.at[spot], k, across_line + half)
+                else:
+                    pltpu.make_async_copy(w.at[x, half], line.at[spot], line_recv.at[k]).start()
+
+    half_back(0, r4a, w2, line2, 3)
+    half_back(1, r4b, w3, line3, 6)
     gather_line(column1, mid1b, full1, 2)
 
     def finish(r, kq):
         q = cols(kq, r)
-        d_norm = dot(proj_ref[...], dproj_s[:, q], NN) + dn_s[:, q]
+        d_norm = dot(projt_s[...], dproj_s[:, q], TN) + dn_s[:, q]
         zhat = zhat_s[:, q]
         m1 = jnp.mean(d_norm, axis=0, keepdims=True)
         m2 = jnp.mean(d_norm * zhat, axis=0, keepdims=True)
@@ -510,10 +540,15 @@
         sent(src, k)
     drain(w1, column1, full1, 0)
     drain(w2, column2, full2, 3)
-    left, right = landed(full2, 5), landed(full3, 8)
-    lower = lax.broadcasted_iota(jnp.int32, left.shape, 1) < hidden
-    proj_out[:, 0:width] = jnp.where(lower, left, pltpu.roll(right, hidden, 1))
-    proj_out[:, width : 2 * width] = jnp.where(lower, pltpu.roll(left, hidden, 1), right)
+    pltpu.make_async_copy(full2, full2, line_recv.at[5]).wait()
+    pltpu.make_async_copy(full3, full3, line_recv.at[8]).wait()
+    for e in range(2):
+        turned = [
+            full[2 * ((x + side // 2) % side) + e].astype(F32)
+            for full in (full2, full3)
+            for x in range(side)
+        ]
+        proj_out[:, e * width : (e + 1) * width] = jnp.concatenate(turned, axis=0).T
     drain(w3, column3, full3, 6)
 
 
@@ -540,6 +575,7 @@
     count = rows * length
     parts = length // LANES
     side = math.isqrt(chips)
+    assert side == 8 and hidden == chips
     share = 2 * side
     vm = pl.BlockSpec(memory_space=pltpu.VMEM)
     hbm = pl.BlockSpec(memory_space=pltpu.HBM)
@@ -556,6 +592,9 @@
             V((block, width), BF16),
             V((share, block, width), BF16),
         ]
+
+    def by_column(block):
+        return [V((side, 2, block, width), BF16), *reduction(block)[1:]]
 
     shapes = (
         jax.ShapeDtypeStruct((count, width), BF16),
@@ -591,19 +630,22 @@
             V((width, count), F32),
             V((hidden, count), BF16),
             V((4 * hidden, count), BF16),
-            V((SLOT * chips, LANES), F32),
+            V((SLOT * chips + 8 * side, LANES), F32),
             V((parts, length, LANES), F32),
             V((2 * pairs * chips, LANES), F32),
             V((rows * chips, length), BF16),
             V((length, length), BF16),
             V((rows * chips, length), BF16),
-            V((SLOT * chips, LANES), F32),
+            V((SLOT * chips + 8 * side, LANES), F32),
             *(13 * [V(slots, BF16)]),
             V((parts, rows * chips, LANES), F32),
             V((parts, rows * chips, LANES), F32),
             *reduction(2 * width // share),
-            *reduction(width // share),
-            *reduction(width // share),
+            V((8 * SLOT, LANES), F32),
+            V((4 * hidden, width), BF16),
+            pltpu.SemaphoreType.DMA((2, side)),
+            *by_column(width // share),
+            *by_column(width // share),
             pltpu.SemaphoreType.DMA((6,)),
             pltpu.SemaphoreType.DMA((6,)),
             pltpu.SemaphoreType.DMA((1 + parts,)),

time: 78.2 us -> 79.1 us (1.012)
  Pallas kernels: 77.5 us -> 78.4 us
    pallas_call x1, Pallas kernels: 76.7 us -> 77.6 us  [local(): pl.pallas_call(kernel, out_shape=shapes, in_specs=8 * [hbm], out_specs=(v...]
where the time goes in v5:
time: 79.1 us; the launch traced here: 79 us
  Pallas kernels  78.4 us (99%)
    pallas_call x1, Pallas kernels, local(): pl.pallas_call(kernel, out_shape=shapes, in_specs=8 * [hbm], out_specs=(v...  77.6 us

profile of v5, /device:TPU:513, one launch (start us, length us, event | category | flops | bytes accessed | tf_op | source)
XLA Modules:
  0.0 79.0 jit_solution(12366388775807349451)
XLA Ops:
  0.6 77.6 %shard_map.111 = (bf16[1152,128]{1,0:T(8,128)(2,1)S(1)}, f32[128,256]{1,0:T(8,128)S(1)}, f32[128,128]{1,0:T(8,128)S(1)}, f32[64,128]{1,0:T(8,128)S(1)}) custom-call(bf16[1152,128]{1,0:T(8,128)(2,1)} %bitcast.3, bf16[1152,128]{1,0:T(8,128)(2,1)} %bitcast.4, s32[3,384]{1,0:T(4,128)} %mask_hbm.1, s32[384]{0:T(512)} %chain_hbm.1, bf16[128,256]{1,0:T(8,128)(2,1)} %proj_hbm.1, ...), custom_call_target="tpu_custom_call" | custom-call | tf_op jit(solution)/shard_map/pallas_call | solution.py:605
  78.2 0.8 %shard_map.112 = (bf16[1152,128]{1,0:T(8,128)(2,1)}, f32[128,256]{1,0:T(8,128)}, f32[128,128]{1,0:T(8,128)}, f32[64,128]{1,0:T(8,128)}) custom-call(bf16[1152,128]{1,0:T(8,128)(2,1)S(1)} %get-tuple-element.12.a_ref, f32[128,256]{1,0:T(8,128)S(1)} %get-tuple-element.13.b_ref, f32[128,128]{1,0:T(8,128)S(1)} %get-tuple-element.14.c_ref, ...), custom_call_target="tpu_custom_call" | custom-call | tf_op jit(solution)/shard_map/pallas_call | solution.py:674

commit v6 on v5

--- a/solution.py
+++ b/solution.py
@@ -152,21 +152,21 @@
 
     barrier = pltpu.get_barrier_semaphore()
 
-    def base_of(i):
+    def line_of(i):
         step = side // 2 + ((i + 1) // 2) * (1 - 2 * lax.rem(i, 2))
-        return lax.rem(row + step, side) * side
+        return lax.rem(row + step, side)
 
     def each_chip(fn, prepare=None):
         def line(i):
-            base, later = base_of(i), base_of(i + 1)
-            for k, d in enumerate(far):
+            now, later = line_of(i), line_of(i + 1)
+            for x, d in enumerate(far):
                 if prepare is not None:
-                    prepare(later + k)
-                fn(base + lax.rem(col + d, side))
+                    prepare(later, x)
+                fn(now * side + lax.rem(col + d, side))
 
         if prepare is not None:
-            for k in range(side):
-                prepare(base_of(jnp.int32(0)) + k)
+            for x in range(side):
+                prepare(line_of(jnp.int32(0)), x)
         loop(side - 1, line)
         for d in far[:-1]:
             fn(row * side + lax.rem(col + d, side))
@@ -180,7 +180,7 @@
     greet(partner)
 
     def exchange(src, dst, k, prepare=None, recv=None):
-        recv = recv_sem.at[k] if recv is None else recv
+        recv = recv_sem.at[k, row] if recv is None else recv
 
         def one(t):
             pltpu.make_async_remote_copy(
@@ -194,9 +194,6 @@
 
         each_chip(one, prepare)
         pltpu.make_async_copy(src.at[chip], dst.at[chip], recv).start()
-
-    def arrive(dst, k):
-        pltpu.make_async_copy(dst, dst, recv_sem.at[k]).wait()
 
     def sent(src, k):
         view = src.at[pl.ds(0, chips - 1)]
@@ -223,26 +220,34 @@
 
     lead = side * SLOT + 8
 
-    def slot(t):
-        return pl.multiple_of(t * SLOT + t // side * 8, 8)
-
-    def unpack(src, dst):
-        def one(t):
-            for i in range(pairs):
-                dst[pl.ds(slot(t) + 2 * i, 2), :] = src[t, i].astype(F32)
-
-        loop(chips, one, unroll=4)
+    def slot(y, x):
+        return pl.multiple_of(y * lead + x * SLOT, 8)
+
+    def unpack(src, dst, k=None, then=None):
+        def one(i):
+            y = line_of(side - 1 - i)
+            line = pl.ds(y * side, side)
+            if k is not None:
+                pltpu.make_async_copy(src.at[line], src.at[line], recv_sem.at[k, y]).wait()
+            if then is not None:
+                then(line)
+            for x in range(side):
+                for i in range(src.shape[1]):
+                    dst[pl.ds(slot(y, x) + 2 * i, 2), :] = src[y * side + x, i].astype(F32)
+
+        loop(side, one)
 
     def pack(src, dst):
-        def one(t):
-            for i in range(pairs):
-                at = pl.ds(slot(t) + 2 * i, 2)
-                dst[t, i] = src[at, :].astype(BF16)
+        def one(y, x):
+            for i in range(dst.shape[1]):
+                at = pl.ds(slot(y, x) + 2 * i, 2)
+                dst[y * side + x, i] = src[at, :].astype(BF16)
 
         return one
 
     def pack_rows(src, dst):
-        def one(t):
+        def one(y, x):
+            t = y * side + x
             for i in range(pairs):
                 dst[t, i] = src[pl.ds(2 * i * chips + t, 2, stride=chips), :].astype(BF16)
 
@@ -254,14 +259,16 @@
     def channels(g, r, kq):
         return pl.ds(g * SLOT + r * parts + kq, 8, stride=lead)
 
-    def gather_rows(src, dst):
-        for r in range(rows):
-            for g in range(0, groups, 2):
-                at = r * chips + g * 8
-                for kq in range(parts):
-                    dst[at : at + 16, kq * LANES : (kq + 1) * LANES] = jnp.concatenate(
-                        [eight(src, g, r, kq), eight(src, g + 1, r, kq)], axis=0
-                    ).astype(BF16)
+    def gather_row(src, dst, r, kq, start):
+        for g in range(0, groups, 2):
+            at = r * chips + g * 8
+            dst[at : at + 16, kq * LANES : (kq + 1) * LANES] = jnp.concatenate(
+                [eight(src, g, 0, start), eight(src, g + 1, 0, start)], axis=0
+            ).astype(BF16)
+
+    def gather_rows(src, dst, n):
+        for k in range(n):
+            gather_row(src, dst, k // parts, k % parts, k)
 
     eye = (
         lax.broadcasted_iota(jnp.int32, (width, width), 0)
@@ -295,10 +302,16 @@
                 (spread, spread2)[ab][
                     channels(g, r, kq), :
                 ] = factors[at : at + 8]
+                if ab == 0 and r == rows - 1:
+                    spread2[channels(g, rows, 0), :] = factors[at : at + 8]
 
     cells(front, unroll=3)
-    loop(chips, pack(spread2, s1b), unroll=4)
-    loop(chips, pack(spread, s1a), unroll=4)
+    def pack_all(y):
+        for src, dst in ((spread2, s1b), (spread, s1a)):
+            for x in range(side):
+                pack(src, dst)(y, x)
+
+    loop(side, pack_all)
     pl.semaphore_wait(barrier, chips + side - 1)
     exchange(s1b, r1b, 0)
     exchange(s1a, r1a, 1)
@@ -331,9 +344,7 @@
             at = 2 * (ab * hidden + x * 8)
             projt_s[at : at + 16, :] = jnp.concatenate(both, axis=0).astype(BF16)
 
-    arrive(r1b, 0)
-    first = to_partner(r1b, r1p, 0)
-    unpack(r1b, spread2)
+    unpack(r1b, spread2, 0, lambda at: to_partner(r1b.at[at], r1p.at[at], 0))
 
     def place_right(src, which):
         for r in range(rows):
@@ -342,12 +353,12 @@
                     wide[kq, pl.ds(g * 48 + 3 * which + r, 8, stride=6), :] = eight(src, g, r, kq)
 
     place_right(spread2, core)
-    first.wait()
+    gather_row(spread2, a_s, rows - 1, parts - 1, rows * parts)
+    pltpu.make_async_copy(r1p, r1p, pair_recv.at[0]).wait()
     unpack(r1p, spread2)
     place_right(spread2, 1 - core)
-    arrive(r1a, 1)
-    unpack(r1a, spread)
-    gather_rows(spread, a_s)
+    unpack(r1a, spread, 1)
+    gather_rows(spread, a_s, rows * parts - 1)
     for kq in range(parts):
         b_s[:, kq * LANES : (kq + 1) * LANES] = wide[kq].astype(BF16)
     for kq in range(parts):
@@ -357,8 +368,7 @@
             flat[at : at + chips, :] = product[r * chips : (r + 1) * chips]
     exchange(s2, r2, 2, pack_rows(flat, s2))
 
-    arrive(r2, 2)
-    unpack(r2, spread)
+    unpack(r2, spread, 2)
 
     def middle(r, kq):
         q = cols(kq, r)
@@ -451,9 +461,8 @@
 
     cells(gate_part, unroll=3)
 
-    arrive(r3, 3)
-    unpack(r3, spread)
-    gather_rows(spread, dt_s)
+    unpack(r3, spread, 3)
+    gather_rows(spread, dt_s, rows * parts)
     second = []
     for kq in range(parts):
         wide[kq] = dot(dt_s[...], a_s[:, kq * LANES : (kq + 1) * LANES], TN)
@@ -512,7 +521,6 @@
 
     half_back(0, r4a, w2, line2, 3)
     half_back(1, r4b, w3, line3, 6)
-    gather_line(column1, mid1b, full1, 2)
 
     def finish(r, kq):
         q = cols(kq, r)
@@ -524,8 +532,9 @@
         pair_out[q, :] = grad.T.astype(BF16)
 
     reduce_column(line2, mid2a, column2, 4)
+    reduce_column(line3, mid3a, column3, 7)
+    gather_line(column1, mid1b, full1, 2)
     cells(finish, unroll=3)
-    reduce_column(line3, mid3a, column3, 7)
     gather_line(column2, mid2b, full2, 5)
 
     def landed(full, k):
@@ -538,6 +547,7 @@
     out_out[...] = sums[width : width + hidden]
     for k, src in enumerate((s1b, s1a, s2, s3, s4a, s4b)):
         sent(src, k)
+    pltpu.make_async_copy(r1p, r1p, pair_send.at[0]).wait()
     drain(w1, column1, full1, 0)
     drain(w2, column2, full2, 3)
     pltpu.make_async_copy(full2, full2, line_recv.at[5]).wait()
@@ -581,7 +591,9 @@
     hbm = pl.BlockSpec(memory_space=pltpu.HBM)
     V = pltpu.VMEM
     pairs = (rows * parts + 1) // 2
+    assert rows * parts == 2 * pairs - 1
     slots = (chips, pairs, 2, LANES)
+    short = (chips, pairs - 1, 2, LANES)
 
     def reduction(block):
         return [
@@ -637,7 +649,10 @@
             V((length, length), BF16),
             V((rows * chips, length), BF16),
             V((SLOT * chips + 8 * side, LANES), F32),
-            *(13 * [V(slots, BF16)]),
+            V(short, BF16),
+            *(5 * [V(slots, BF16)]),
+            V(short, BF16),
+            *(6 * [V(slots, BF16)]),
             V((parts, rows * chips, LANES), F32),
             V((parts, rows * chips, LANES), F32),
             *reduction(2 * width // share),
@@ -647,7 +662,7 @@
             *by_column(width // share),
             *by_column(width // share),
             pltpu.SemaphoreType.DMA((6,)),
-            pltpu.SemaphoreType.DMA((6,)),
+            pltpu.SemaphoreType.DMA((4, side)),
             pltpu.SemaphoreType.DMA((1 + parts,)),
             pltpu.SemaphoreType.DMA((1 + parts,)),
             pltpu.SemaphoreType.DMA((9,)),

time: 79.1 us -> 78.1 us (0.987)
  Pallas kernels: 78.4 us -> 77.4 us
    pallas_call x1, Pallas kernels: 77.6 us -> 76.6 us  [local(): pl.pallas_call(kernel, out_shape=shapes, in_specs=8 * [hbm], out_specs=(v...]
where the time goes in v6:
time: 78.1 us; the launch traced here: 78 us
  Pallas kernels  77.4 us (99%)
    pallas_call x1, Pallas kernels, local(): pl.pallas_call(kernel, out_shape=shapes, in_specs=8 * [hbm], out_specs=(v...  76.6 us

profile of v6, /device:TPU:513, one launch (start us, length us, event | category | flops | bytes accessed | tf_op | source)
XLA Modules:
  0.0 78.0 jit_solution(6587096282017773911)
XLA Ops:
  0.6 76.6 %shard_map.111 = (bf16[1152,128]{1,0:T(8,128)(2,1)S(1)}, f32[128,256]{1,0:T(8,128)S(1)}, f32[128,128]{1,0:T(8,128)S(1)}, f32[64,128]{1,0:T(8,128)S(1)}) custom-call(bf16[1152,128]{1,0:T(8,128)(2,1)} %bitcast.3, bf16[1152,128]{1,0:T(8,128)(2,1)} %bitcast.4, s32[3,384]{1,0:T(4,128)} %mask_hbm.1, s32[384]{0:T(512)} %chain_hbm.1, bf16[128,256]{1,0:T(8,128)(2,1)} %proj_hbm.1, ...), custom_call_target="tpu_custom_call" | custom-call | tf_op jit(solution)/shard_map/pallas_call | solution.py:617
  77.2 0.8 %shard_map.112 = (bf16[1152,128]{1,0:T(8,128)(2,1)}, f32[128,256]{1,0:T(8,128)}, f32[128,128]{1,0:T(8,128)}, f32[64,128]{1,0:T(8,128)}) custom-call(bf16[1152,128]{1,0:T(8,128)(2,1)S(1)} %get-tuple-element.12.a_ref, f32[128,256]{1,0:T(8,128)S(1)} %get-tuple-element.13.b_ref, f32[128,128]{1,0:T(8,128)S(1)} %get-tuple-element.14.c_ref, ...), custom_call_target="tpu_custom_call" | custom-call | tf_op jit(solution)/shard_map/pallas_call | solution.py:689

commit v7 on v6

--- a/solution.py
+++ b/solution.py
@@ -490,8 +490,10 @@
     exchange(s4b, r4b, 5, pack_rows(flat, s4b), col_recv.at[1, col])
     reduce_column(line1, mid1a, column1, 1)
 
-    def half_back(ab, src, w, line, k):
+    def half_back(ab, src, w, line, k, ahead=None):
         for d in reversed(far):
+            if ahead is not None and d == side // 2:
+                ahead()
             x = lax.rem(col + d, side)
             view = src.at[pl.ds(0, side)]
             pltpu.make_async_copy(view, view, col_recv.at[ab, x]).wait()
@@ -520,7 +522,7 @@
                     pltpu.make_async_copy(w.at[x, half], line.at[spot], line_recv.at[k]).start()
 
     half_back(0, r4a, w2, line2, 3)
-    half_back(1, r4b, w3, line3, 6)
+    half_back(1, r4b, w3, line3, 6, lambda: reduce_column(line2, mid2a, column2, 4))
 
     def finish(r, kq):
         q = cols(kq, r)
@@ -531,7 +533,6 @@
         grad = zscale_s[:, q] * (d_norm - m1 - zhat * m2)
         pair_out[q, :] = grad.T.astype(BF16)
 
-    reduce_column(line2, mid2a, column2, 4)
     reduce_column(line3, mid3a, column3, 7)
     gather_line(column1, mid1b, full1, 2)
     cells(finish, unroll=3)

time: 78.1 us -> 78.1 us (level)
  no operation moved by 1% of the time
where the time goes in v7:
time: 78.1 us; the launch traced here: 78 us
  Pallas kernels  77.4 us (99%)
    pallas_call x1, Pallas kernels, local(): pl.pallas_call(kernel, out_shape=shapes, in_specs=8 * [hbm], out_specs=(v...  76.6 us

profile of v7, /device:TPU:513, one launch (start us, length us, event | category | flops | bytes accessed | tf_op | source)
XLA Modules:
  0.0 78.0 jit_solution(17798982831811740013)
XLA Ops:
  0.6 76.6 %shard_map.111 = (bf16[1152,128]{1,0:T(8,128)(2,1)S(1)}, f32[128,256]{1,0:T(8,128)S(1)}, f32[128,128]{1,0:T(8,128)S(1)}, f32[64,128]{1,0:T(8,128)S(1)}) custom-call(bf16[1152,128]{1,0:T(8,128)(2,1)} %bitcast.3, bf16[1152,128]{1,0:T(8,128)(2,1)} %bitcast.4, s32[3,384]{1,0:T(4,128)} %mask_hbm.1, s32[384]{0:T(512)} %chain_hbm.1, bf16[128,256]{1,0:T(8,128)(2,1)} %proj_hbm.1, ...), custom_call_target="tpu_custom_call" | custom-call | tf_op jit(solution)/shard_map/pallas_call | solution.py:618
  77.2 0.8 %shard_map.112 = (bf16[1152,128]{1,0:T(8,128)(2,1)}, f32[128,256]{1,0:T(8,128)}, f32[128,128]{1,0:T(8,128)}, f32[64,128]{1,0:T(8,128)}) custom-call(bf16[1152,128]{1,0:T(8,128)(2,1)S(1)} %get-tuple-element.12.a_ref, f32[128,256]{1,0:T(8,128)S(1)} %get-tuple-element.13.b_ref, f32[128,128]{1,0:T(8,128)S(1)} %get-tuple-element.14.c_ref, ...), custom_call_target="tpu_custom_call" | custom-call | tf_op jit(solution)/shard_map/pallas_call | solution.py:690
